TPU v7x, 256 devices: a whole 4x4x8 slice. The times are simulated.
256 devices in a mesh: aa: 64 (over y, z, core), ba: 4 (over x).
Axes of the slice: x: 4, y: 4, z: 8, core: 2. Of those that a mesh axis runs over, the one named last changes fastest.
Arguments:
- inputs: bfloat16 [32768, 3584], P('aa', 'ba'), may hold values from -6 to 6
- cotangent: bfloat16 [32768, 3584], P('aa', 'ba'), may hold values from -6 to 6
- base_weight: bfloat16 [3584, 3584], P(None, 'ba'), may hold values from -0.09375 to 0.09375
- adapter_ids: int32 [32768, 1], P('aa'), may hold values from 0 to 255; in each aligned block of 512 rows (0 to 511, 512 to 1023, ...) at most 4 rows name the same one
- adapters: float32 [256, 2, 16, 3584], P('aa', None, None, 'ba'), may hold values from -0.09375 to 0.09375
- first_moment: float32 [256, 2, 16, 3584], P('aa', None, None, 'ba'), may hold values from -3 to 3
- second_moment: float32 [256, 2, 16, 3584], P('aa', None, None, 'ba'), may hold values from 0.05 to 1
Outputs:
- input_gradient: bfloat16 [32768, 3584], P('aa', 'ba')
- new_adapters: float32 [256, 2, 16, 3584], P('aa', None, None, 'ba')
- new_first: float32 [256, 2, 16, 3584], P('aa', None, None, 'ba')
- new_second: float32 [256, 2, 16, 3584], P('aa', None, None, 'ba')
- grad_norm: float32 [], replicated
Inputs may be any that keep to these rules, and one draw needn't show every extreme that they name: `adapter_ids`: in the rows of one device no adapter is named by more than 4 tokens, a bound that some block reaches; every adapter is named somewhere.
All inputs are finite; a program needn't handle non-finite values.
Results may differ from a plain program's by a relative error of at most 0.0034.
Values may be sent and summed in bfloat16 or wider, within the bound.
A program may use at most 128 MiB of HBM per device.

v0:
```python
import math

import jax
import jax.numpy as jnp
from jax import lax
from jax.sharding import PartitionSpec as P

MODEL_WIDTH = 3584
R = 16


adapter_scale = 2.0
beta_first = 0.9
beta_second = 0.999
adam_eps = 1e-08
learn_rate = 0.01
bias_first = 1.0 - math.exp(1000.0 * math.log(beta_first))
bias_second = 1.0 - math.exp(1000.0 * math.log(beta_second))


def sent_together(arrays, axis, split_dim, concat_dim, along):
    widths = [a.shape[along] for a in arrays]
    both = jnp.concatenate(arrays, axis=along)
    result = lax.all_to_all(both, axis, split_axis=split_dim, concat_axis=concat_dim, tiled=True)
    return tuple(jnp.split(result, [sum(widths[:k]) for k in range(1, len(widths))], axis=along))


def copy_for_each(shard, axis):
    copies = jnp.broadcast_to(shard, (lax.axis_size(axis), *shard.shape))
    return lax.all_to_all(copies, axis, split_axis=0, concat_axis=0, tiled=True)


def of_everyone(shard, axis):
    everything = copy_for_each(shard, axis)
    return jnp.sum(everything, axis=0)


def packed_total(arrays, axis):
    ends = [0]
    for a in arrays:
        ends.append(ends[-1] + a.size)
    running = of_everyone(jnp.concatenate([a.ravel() for a in arrays]), axis)
    return tuple((running[b:e].reshape(a.shape) for a, b, e in zip(arrays, ends, ends[1:])))


def adam_update(adapters, first_moment, second_moment, gradients, squares):
    clip_limit = math.sqrt(2.0 * R * MODEL_WIDTH)
    clip_factor = clip_limit / jnp.maximum(jnp.sqrt(squares), clip_limit)
    clipped = gradients * clip_factor[:, None, None, None]
    new_first = beta_first * first_moment + (1.0 - beta_first) * clipped
    new_second = beta_second * second_moment + (1.0 - beta_second) * clipped * clipped
    update = new_first / bias_first / (jnp.sqrt(new_second / bias_second) + adam_eps)
    return (adapters - learn_rate * update, new_first, new_second)


def local(inputs, cotangent, base_weight, adapter_ids, adapters, first_moment, second_moment):
    tok_rows, feature_width = inputs.shape
    owners = lax.axis_size("aa")
    local_count = adapters.shape[0]
    adapter_total = owners * local_count
    capacity = max(2, 2 * tok_rows // adapter_total)
    holding_rows = adapter_total * capacity
    chosen = adapter_ids[:, 0]
    counter = jnp.arange(tok_rows, dtype=jnp.int32)
    matches = (chosen[:, None] == chosen[None, :]) & (counter[None, :] < counter[:, None])
    slot_rank = jnp.sum(matches.astype(jnp.int32), axis=1)
    token_position = chosen * capacity + slot_rank
    send_inputs = (
        jnp.zeros((holding_rows, feature_width), jnp.bfloat16).at[token_position].set(inputs)
    )
    send_cotangent = (
        jnp.zeros((holding_rows, feature_width), jnp.bfloat16).at[token_position].set(cotangent)
    )
    recv_inputs, recv_cotangent = sent_together((send_inputs, send_cotangent), "aa", 0, 0, 1)
    grid_shape = (owners, local_count, capacity, feature_width)
    recv_inputs = recv_inputs.reshape(grid_shape)
    recv_cotangent = recv_cotangent.reshape(grid_shape)
    down_reduced = adapters[:, 0].astype(jnp.bfloat16)
    up_low = adapters[:, 1].astype(jnp.bfloat16)
    projected = jnp.einsum(
        "slkd,lrd->slkr", recv_inputs, down_reduced, preferred_element_type=jnp.float32
    )
    pulled = jnp.einsum(
        "slkd,lrd->slkr", recv_cotangent, up_low, preferred_element_type=jnp.float32
    )
    projected, pulled = packed_total((projected, pulled), "ba")
    projection_reduced = projected.astype(jnp.bfloat16)
    fetched_reduced = pulled.astype(jnp.bfloat16)
    down_gradient = adapter_scale * jnp.einsum(
        "slkr,slkd->lrd", fetched_reduced, recv_inputs, preferred_element_type=jnp.float32
    )
    up_gradient = adapter_scale * jnp.einsum(
        "slkr,slkd->lrd", projection_reduced, recv_cotangent, preferred_element_type=jnp.float32
    )
    adapter_rows = (
        adapter_scale
        * jnp.einsum(
            "slkr,lrd->slkd", fetched_reduced, down_reduced, preferred_element_type=jnp.float32
        )
    ).astype(jnp.bfloat16)
    gathered_result = lax.all_to_all(
        adapter_rows.reshape(holding_rows, feature_width),
        "aa",
        split_axis=0,
        concat_axis=0,
        tiled=True,
    )
    adapter_local = gathered_result[token_position]
    partial_sums = lax.dot_general(
        cotangent, base_weight, (((1,), (1,)), ((), ())), preferred_element_type=jnp.float32
    )
    frozen_term = lax.psum_scatter(partial_sums, "ba", scatter_dimension=1, tiled=True)
    input_gradient = (frozen_term + adapter_local.astype(jnp.float32)).astype(jnp.bfloat16)
    gradients = jnp.stack([down_gradient, up_gradient], axis=1)
    part_squares = jnp.sum(gradients * gradients, axis=(1, 2, 3))
    squares = of_everyone(part_squares, "ba")
    grand_total = of_everyone(jnp.sum(squares), "aa")
    new_adapters, new_first, new_second = adam_update(
        adapters, first_moment, second_moment, gradients, squares
    )
    return (input_gradient, new_adapters, new_first, new_second, jnp.sqrt(grand_total))


def solution(mesh):
    in_specs = (
        P("aa", "ba"),
        P("aa", "ba"),
        P(None, "ba"),
        P("aa", None),
        P("aa", None, None, "ba"),
        P("aa", None, None, "ba"),
        P("aa", None, None, "ba"),
    )
    out_specs = (
        P("aa", "ba"),
        P("aa", None, None, "ba"),
        P("aa", None, None, "ba"),
        P("aa", None, None, "ba"),
        P(),
    )
    return jax.shard_map(local, mesh=mesh, in_specs=in_specs, out_specs=out_specs, check_vma=False)
```

profile of v0, /device:TPU:1, one launch (start us, length us, event | category | flops | bytes accessed | tf_op | source)
XLA Modules:
  0.0 245.1 jit_solution(2643552713090840868)
XLA Ops:
  7.2 0.0 reduce-scatter.2.cloned.1.call-start
  7.2 10.1 %fusion.45 = f32[512,3584]{1,0:T(8,128)} fusion(bf16[512,896]{1,0:T(8,128)(2,1)} %param.8, bf16[3584,896]{1,0:T(8,128)(2,1)} %param.9), kind=kOutput, calls=%fused_computation.48 | convolution fusion | flops 3288334336 | bytes 14680064 | tf_op jit(solution)/shard_map/dot_general | solution.py:109
  17.3 0.0 copy-start.3
  17.3 0.0 reduce-scatter.2.cloned.1.call-update
  17.3 0.7 copy-done.3
  18.0 0.2 convert_reduce_fusion
  18.2 3.7 %scatter_custom_fusion.1 = bf16[1024,896]{1,0:T(8,128)(2,1)S(1)} fusion(s32[512]{0:T(512)S(1)} %bitcast.55, bf16[512,896]{1,0:T(8,128)(2,1)} %param.8, bf16[]{:T(256)} %constant.14.clone.1), kind=kCustom, calls=%fused_computation.25 | custom fusion | bytes 1835520 | tf_op jit(solution)/shard_map/scatter | solution.py:72
  22.0 4.6 %scatter_custom_fusion = bf16[1024,896]{1,0:T(8,128)(2,1)} fusion(s32[512]{0:T(512)S(1)} %bitcast.56, bf16[512,896]{1,0:T(8,128)(2,1)} %param.7, bf16[]{:T(256)} %constant.14.clone.1), kind=kCustom, calls=%fused_computation.27 | custom fusion | bytes 1835520 | tf_op jit(solution)/shard_map/scatter | solution.py:69
  26.6 1.8 pad_maximum_fusion
  28.3 97.6 %all_to_all.42 = bf16[64,16,1792]{2,1,0:T(8,128)(2,1)S(1)} all-to-all(bf16[64,16,1792]{2,1,0:T(8,128)(2,1)S(1)} %bitcast.52), channel_id=1, replica_groups=mesh['aa'=64,'ba'=4] {'aa'}, dimensions={0} | all-to-all | bytes 7340032 | tf_op jit(solution)/shard_map/all_to_all | solution.py:24
  126.0 1.5 fusion.43
  127.5 4.2 %reshape.69 = bf16[64,4,4,896]{3,2,1,0:T(4,128)(2,1)} reshape(bf16[1024,896]{1,0:T(8,128)(2,1)} %get-tuple-element.36) | data formatting | bytes 3670016 | tf_op jit(solution)/shard_map/reshape | solution.py:77
  131.7 0.0 copy-done.1
  131.7 2.4 fusion.29
  134.2 0.4 copy.75
  134.5 0.3 reshape.70
  134.9 1.5 reshape.67
  136.3 2.4 fusion.26
  138.8 0.4 copy.73
  139.1 0.3 reshape.68
  139.5 0.3 broadcast_in_dim.6
  139.8 13.0 %all_to_all.43 = f32[4,1,32768]{2,1,0:T(1,128)S(1)} all-to-all(f32[4,1,32768]{2,1,0:T(1,128)S(1)} %broadcast_in_dim.6), channel_id=1, replica_groups=mesh['aa'=64,'ba'=4] {'ba'}, dimensions={0} | all-to-all | bytes 1048576 | tf_op jit(solution)/shard_map/all_to_all | solution.py:30
  152.8 0.6 reduce_sum.58
  153.4 0.2 convert_element_type.34
  153.6 0.3 copy.77
  153.9 0.2 convert_element_type.39
  154.1 1.9 fusion.17
  156.0 0.0 copy-done
  156.0 0.4 fusion.23
  156.5 0.1 multiply_reduce_fusion
  156.6 6.5 %all_to_all.44 = f32[4,1,4]{2,1,0:T(1,128)S(1)} all-to-all(f32[4,1,4]{2,1,0:T(1,128)S(1)} %broadcast_in_dim.7), channel_id=1, replica_groups=mesh['aa'=64,'ba'=4] {'ba'}, dimensions={0} | all-to-all | bytes 128 | tf_op jit(solution)/shard_map/all_to_all | solution.py:30
  163.1 0.6 fusion.40
  163.7 1.3 broadcast_in_dim.8
  164.9 8.0 %all-to-all-start.4 = ((f32[64,1,1]{2,1,0:T(1,128)}), f32[64,1,1]{2,1,0:T(1,128)S(1)}, u32[]{:S(2)}, u32[]{:S(2)}) async-start(f32[64,1,1]{2,1,0:T(1,128)} %broadcast_in_dim.8), calls=%async_computation.5 | async-start | bytes 65536 | tf_op jit(solution)/shard_map/all_to_all | solution.py:30
  172.9 0.7 multiply_convert_fusion
  173.6 2.3 copy.78
  175.9 6.3 %all-to-all-done.4 = f32[64,1,1]{2,1,0:T(1,128)S(1)} async-done(((f32[64,1,1]{2,1,0:T(1,128)}), f32[64,1,1]{2,1,0:T(1,128)S(1)}, u32[]{:S(2)}, u32[]{:S(2)}) %all-to-all-start.4) | async-done | bytes 288 | tf_op jit(solution)/shard_map/all_to_all | solution.py:30
  182.2 4.8 %all-to-all-start.2 = ((bf16[64,16,896]{2,1,0:T(8,128)(2,1)}), bf16[64,16,896]{2,1,0:T(8,128)(2,1)S(1)}, u32[]{:S(2)}, u32[]{:S(2)}) async-start(bf16[64,16,896]{2,1,0:T(8,128)(2,1)} %copy.78), calls=%async_computation.3 | async-start | bytes 3670016 | tf_op jit(solution)/shard_map/all_to_all | solution.py:101
  187.0 0.0 copy-done.2
  187.0 1.4 multiply_subtract_fusion
  188.4 0.8 copy.89
  189.2 0.8 copy.90
  190.0 0.8 copy.91
  190.8 0.7 reduce_sum.62
  192.2 40.3 %all-to-all-done.2 = bf16[64,16,896]{2,1,0:T(8,128)(2,1)S(1)} async-done(((bf16[64,16,896]{2,1,0:T(8,128)(2,1)}), bf16[64,16,896]{2,1,0:T(8,128)(2,1)S(1)}, u32[]{:S(2)}, u32[]{:S(2)}) %all-to-all-start.2) | async-done | bytes 1835040 | tf_op jit(solution)/shard_map/all_to_all | solution.py:101
  232.4 2.0 gather_fusion
  234.5 0.0 reduce-scatter.2.cloned.1.call-done
  234.5 2.6 %add_convert_fusion = bf16[512,896]{1,0:T(8,128)(2,1)} fusion(f32[512,896]{1,0:T(8,128)} %reduce-scatter.2.cloned.1.call-done, bf16[512,896]{1,0:T(8,128)(2,1)S(1)} %gather_fusion), kind=kLoop, calls=%fused_computation.5 | loop fusion | flops 1376256 | bytes 3670016 | tf_op jit(solution)/shard_map/convert_element_type | solution.py:113
  (9 shorter events, 0.1 us)
Async XLA Ops:
  7.2 227.3 %reduce-scatter.2.cloned.1.call-start = ((), (), s32[]{:S(2)}) async-start(), calls=%async_computation.6 | async-start | bytes 9175040 | tf_op jit(solution)/shard_map/reduce_scatter | solution.py:112
  17.3 0.7 copy-start.3
  127.5 4.2 %copy-start.1 = (f32[4,2,16,896]{3,2,1,0:T(8,128)S(1)}, f32[4,2,16,896]{3,2,1,0:T(8,128)}, u32[]{:S(2)}) copy-start(f32[4,2,16,896]{3,2,1,0:T(8,128)} %param.11) | copy-start | bytes 1376260
  152.8 3.2 %copy-start = (bf16[64,4,4,896]{3,2,1,0:T(4,128)(2,1)S(1)}, bf16[64,4,4,896]{3,2,1,0:T(4,128)(2,1)}, u32[]{:S(2)}) copy-start(bf16[64,4,4,896]{3,2,1,0:T(4,128)(2,1)} %reshape.69) | copy-start | bytes 5505028
  164.9 17.2 %all-to-all-start.4 = ((f32[64,1,1]{2,1,0:T(1,128)}), f32[64,1,1]{2,1,0:T(1,128)S(1)}, u32[]{:S(2)}, u32[]{:S(2)}) async-start(f32[64,1,1]{2,1,0:T(1,128)} %broadcast_in_dim.8), calls=%async_computation.5 | async-start | bytes 65536 | tf_op jit(solution)/shard_map/all_to_all | solution.py:30
  175.9 11.1 %copy-start.2 = (f32[4,2,16,896]{3,2,1,0:T(8,128)S(1)}, f32[4,2,16,896]{3,2,1,0:T(8,128)}, u32[]{:S(2)}) copy-start(f32[4,2,16,896]{3,2,1,0:T(8,128)} %param.13) | copy-start | bytes 1376260
  182.2 50.3 %all-to-all-start.2 = ((bf16[64,16,896]{2,1,0:T(8,128)(2,1)}), bf16[64,16,896]{2,1,0:T(8,128)(2,1)S(1)}, u32[]{:S(2)}, u32[]{:S(2)}) async-start(bf16[64,16,896]{2,1,0:T(8,128)(2,1)} %copy.78), calls=%async_computation.3 | async-start | bytes 3670016 | tf_op jit(solution)/shard_map/all_to_all | solution.py:101
Sparse Core Ops, SparseCore 0:
  17.4 78.7 reduce-scatter.1
where the time goes:
time: 246 us; the launch traced here: 245 us
  blocking collectives  117 us (48%)
  waiting for transfers between devices  46.6 us (19%)
  local copies, waits for them, and re-layouts  26.6 us (11%)
  matrix products  17.9 us (7%)
  between operations  16 us (7%)
  starting transfers between devices  12.8 us (5%)
  other arithmetic  8.07 us (3%)
    all_to_all x1, blocking collectives, sent_together(): lax.all_to_all(both, axis, split_axis=split_dim, concat_axis=concat_dim,...  97.6 us
    all_to_all x1, waiting for transfers between devices, local(): lax.all_to_all(adapter_rows.reshape(holding_rows, feature_width), 'aa', s...  40.3 us
    all_to_all x2, blocking collectives, copy_for_each(): return lax.all_to_all(copies, axis, split_axis=0, concat_axis=0, tiled=True)  19.5 us
    dot_general x1, matrix products, local(): lax.dot_general(cotangent, base_weight, (((1,), (1,)), ((), ())), preferr...  10.1 us
    scatter x2, local copies, waits for them, and re-layouts, local(): jnp.zeros((holding_rows, feature_width), jnp.bfloat16).at[token_position]  8.33 us
    all_to_all x1, starting transfers between devices, copy_for_each(): return lax.all_to_all(copies, axis, split_axis=0, concat_axis=0, tiled=True)  7.98 us
    all_to_all x1, waiting for transfers between devices, copy_for_each(): return lax.all_to_all(copies, axis, split_axis=0, concat_axis=0, tiled=True)  6.27 us
  transfers between devices with their start and end apart: 3, of which 2 were waited for; matrix products, arithmetic and copies ran while one was open for 16% of the time, Pallas kernels for 0%

commit v1 on v0

v1 whole, which is shorter than its diff:
```python
import math

import jax
import jax.numpy as jnp
from jax import lax
from jax.experimental import pallas as pl
from jax.experimental.pallas import tpu as pltpu
from jax.sharding import PartitionSpec as P

MODEL_WIDTH = 3584
R = 16
NY, NZ, NC, NX = 4, 8, 2, 4
NK = 4
MOST = 4
GROUP = NY * NC
CHUNK = NZ * MOST
MESH = pl.DeviceIdType.MESH

adapter_scale = 2.0
beta_first = 0.9
beta_second = 0.999
adam_eps = 1e-08
learn_rate = 0.01
bias_first = 1.0 - math.exp(1000.0 * math.log(beta_first))
bias_second = 1.0 - math.exp(1000.0 * math.log(beta_second))

EX = ((2, 0), (2, 1), (1, 0), (3, 0), (1, 1), (3, 1), (0, 1))
ZOFF = (4, 3, 5, 2, 6, 1, 7)
XOFF = (2, 1, 3)


def adam_update(adapters, first_moment, second_moment, gradients, squares):
    clip_limit = math.sqrt(2.0 * R * MODEL_WIDTH)
    clip_factor = clip_limit / jnp.maximum(jnp.sqrt(squares), clip_limit)
    clipped = gradients * clip_factor[:, None, None, None]
    new_first = beta_first * first_moment + (1.0 - beta_first) * clipped
    new_second = beta_second * second_moment + (1.0 - beta_second) * clipped * clipped
    update = new_first / bias_first / (jnp.sqrt(new_second / bias_second) + adam_eps)
    return (adapters - learn_rate * update, new_first, new_second)


def nt(a, b):
    return lax.dot_general(a, b, (((1,), (1,)), ((), ())), preferred_element_type=jnp.float32)


def nn(a, b):
    return jnp.dot(a, b, preferred_element_type=jnp.float32)


def kernel(
    posr, posc, x_hbm, g_hbm, w_hbm, adf,
    out_ref, grad_ref, st_ref,
    xg, w, snd, rcv, adb, bs, br, acc, cs, cr, ls, lr, gs, gr, gf, sqs, sqr, ts, ty, us, tz,
    lsem, ex_s, ex_r, ag_s, ag_r, b_s, b_r, c_s, c_r, l_s, l_r, g_s, g_r, q_s, q_r, y_s, y_r, z_s, z_r,
):
    a = lax.axis_index("aa")
    x = lax.axis_index("ba")
    y, z, c = a // (NZ * NC), (a // NC) % NZ, a % NC
    me = y * NC + c
    fw = x_hbm.shape[1]

    def at_yc(dy, dc):
        yy, cc = (y + dy) % NY, (c + dc) % NC
        return yy * NC + cc, ((yy * NZ + z) * NC + cc, x)

    def at_z(dz):
        zz = (z + dz) % NZ
        return zz, ((y * NZ + zz) * NC + c, x)

    def at_x(dx):
        xx = (x + dx) % NX
        return xx, (a, xx)

    def remote(src, dst, ssem, rsem, dev):
        return pltpu.make_async_remote_copy(
            src_ref=src, dst_ref=dst, send_sem=ssem, recv_sem=rsem, device_id=dev, device_id_type=MESH
        )

    loads = [
        pltpu.make_async_copy(x_hbm, xg.at[:, 0:fw], lsem.at[0]),
        pltpu.make_async_copy(g_hbm, xg.at[:, fw : 2 * fw], lsem.at[1]),
        pltpu.make_async_copy(w_hbm, w, lsem.at[2]),
    ]
    for cp in loads:
        cp.start()

    barrier = pltpu.get_barrier_semaphore()
    for dy, dc in EX:
        pl.semaphore_signal(barrier, inc=1, device_id=at_yc(dy, dc)[1], device_id_type=MESH)
    for dz in ZOFF:
        pl.semaphore_signal(barrier, inc=1, device_id=at_z(dz)[1], device_id_type=MESH)
    for dx in XOFF:
        pl.semaphore_signal(barrier, inc=1, device_id=at_x(dx)[1], device_id_type=MESH)

    for k in range(NK):
        adb[k, z] = adf[k].astype(jnp.bfloat16)

    def ex_copy(k, j):
        d, dev = at_yc(*EX[j])
        return remote(snd.at[k, d], rcv.at[k, me], ex_s.at[k, j], ex_r.at[k, j], dev)

    def lora_copy(k, j):
        d, dev = at_yc(*EX[j])
        return remote(ls.at[k, d], lr.at[k, me], l_s.at[k, j], l_r.at[k, j], dev)

    def ag_copy(k, s, up):
        if up:
            o = (z - s + NZ) % NZ
            return remote(adb.at[k, o], adb.at[k, o], ag_s.at[k, s], ag_r.at[k, s], at_z(1)[1])
        o = (z + s) % NZ
        return remote(adb.at[k, o], adb.at[k, o], ag_s.at[k, 4 + s], ag_r.at[k, 4 + s], at_z(NZ - 1)[1])

    def g_copy(k, j):
        zz, dev = at_z(ZOFF[j])
        return remote(gs.at[k, zz], gr.at[k, j], g_s.at[k, j], g_r.at[k, j], dev)

    def base_copy(k, j):
        return remote(bs.at[k, j], br.at[k, j], b_s.at[k, j], b_r.at[k, j], at_x(XOFF[j])[1])

    def c_copy(k, j):
        return remote(cs.at[k], cr.at[k, x], c_s.at[k, j], c_r.at[k, j], at_x(XOFF[j])[1])

    def gather(k):
        rows = lax.broadcasted_iota(jnp.int32, (GROUP * CHUNK, 1), 0) + k * (GROUP * CHUNK)
        hot = jnp.where(rows == posr[...], 1.0, 0.0).astype(jnp.bfloat16)
        got = nn(hot, xg[...]).astype(jnp.bfloat16).reshape(GROUP, CHUNK, 2 * fw)
        snd[k] = got
        rcv[k, me] = snd[k, me]

    def send_tokens(k):
        for j in range(len(EX)):
            ex_copy(k, j).start()

    def base(k):
        rows = acc.shape[0] // NK
        here = pl.ds(pl.multiple_of(k * rows, rows), rows)
        g = xg[here, fw : 2 * fw]
        for j, dx in enumerate(XOFF):
            xx = at_x(dx)[0]
            part = nt(g, w[pl.ds(pl.multiple_of(xx * fw, fw), fw), :])
            bs[k, j] = part.astype(jnp.bfloat16)
            base_copy(k, j).start()
        acc[here, :] = nt(g, w[pl.ds(pl.multiple_of(x * fw, fw), fw), :])

    loads[0].wait()
    loads[1].wait()
    gather(0)
    pl.semaphore_wait(barrier, len(EX) + len(ZOFF) + len(XOFF))

    def ag_ways(k, s):
        return [up for up in (True, False) if s < 3 or up == (k % 2 == 0)]

    def ag_pass(s):
        for k in range(NK):
            for up in ag_ways(k, s):
                if s > 0:
                    ag_copy(k, s - 1, up).wait_recv()
                ag_copy(k, s, up).start()

    ag_pass(0)
    send_tokens(0)

    def feed(k, carry):
        gather(k)
        send_tokens(k)
        return carry

    lax.fori_loop(1, NK, feed, 0)
    ag_pass(1)
    loads[2].wait()
    base(0)
    ag_pass(2)
    ag_pass(3)
    for k in range(NK):
        for up in (True, False):
            last = 3 if up in ag_ways(k, 3) else 2
            for s in ((last,) if last == 3 else ()):
                ag_copy(k, s, up).wait_recv()
            if last == 2:
                ag_copy(k, 2, up).wait_recv()

    lane = lax.broadcasted_iota(jnp.int32, (1, NZ, NZ * R), 2) // R
    sub = lax.broadcasted_iota(jnp.int32, (1, NZ, NZ * R), 1)
    mine = lane == sub
    nrow = GROUP * CHUNK

    def step(k, carry):
        for j in range(len(EX)):
            ex_copy(k, j).wait_recv()
        down = adb[k, :, 0].reshape(NZ * R, fw)
        up = adb[k, :, 1].reshape(NZ * R, fw)
        xs = rcv[k, :, :, 0:fw].reshape(nrow, fw)
        gg = rcv[k, :, :, fw : 2 * fw].reshape(nrow, fw)
        pulled = nt(gg, up).reshape(GROUP * MOST, NZ, NZ * R)
        projected = nt(xs, down).reshape(GROUP * MOST, NZ, NZ * R)
        cs[k, 0] = jnp.sum(jnp.where(mine, pulled, 0.0), axis=1)
        cs[k, 1] = jnp.sum(jnp.where(mine, projected, 0.0), axis=1)
        cr[k, x] = cs[k]
        for j in range(len(XOFF)):
            c_copy(k, j).start()

        @pl.when(k < NK - 1)
        def _():
            base(k + 1)

        for j in range(len(XOFF)):
            c_copy(k, j).wait_recv()
        total = cr[k, 0] + cr[k, 1] + cr[k, 2] + cr[k, 3]
        low = total.astype(jnp.bfloat16).astype(jnp.float32)
        pull = jnp.where(mine, low[0][:, None, :], 0.0).reshape(nrow, NZ * R)
        proj = jnp.where(mine, low[1][:, None, :], 0.0).reshape(nrow, NZ * R)
        gd = adapter_scale * nn(pull.T.astype(jnp.bfloat16), xs)
        gu = adapter_scale * nn(proj.T.astype(jnp.bfloat16), gg)
        gf[:, 0] = gd.reshape(NZ, R, fw)
        gf[:, 1] = gu.reshape(NZ, R, fw)
        gs[k, :, 0] = gd.reshape(NZ, R, fw).astype(jnp.bfloat16)
        gs[k, :, 1] = gu.reshape(NZ, R, fw).astype(jnp.bfloat16)
        for j in range(len(ZOFF)):
            g_copy(k, j).start()
        grad_ref[k] = gf[z]
        lora = adapter_scale * nn(pull.astype(jnp.bfloat16), down)
        ls[k] = lora.astype(jnp.bfloat16).reshape(GROUP, CHUNK, fw)
        for j in range(len(EX)):
            lora_copy(k, j).start()
        lr[k, me] = ls[k, me]
        return carry

    lax.fori_loop(0, NK, step, 0)

    def frozen(k, carry):
        rows = acc.shape[0] // NK
        here = pl.ds(pl.multiple_of(k * rows, rows), rows)
        t = acc[here, :]
        for j in range(len(XOFF)):
            base_copy(k, j).wait_recv()
        for j in range(len(XOFF)):
            t = t + br[k, j].astype(jnp.float32)
        acc[here, :] = t
        return carry

    lax.fori_loop(0, NK, frozen, 0)

    def unslot(k, carry):
        for j in range(len(EX)):
            lora_copy(k, j).wait_recv()
        cols = lax.broadcasted_iota(jnp.int32, (1, nrow), 1) + k * nrow
        hot = jnp.where(posc[...] == cols, 1.0, 0.0).astype(jnp.bfloat16)
        acc[...] += nn(hot, lr[k].reshape(nrow, fw))
        return carry

    lax.fori_loop(0, NK, unslot, 0)
    out_ref[...] = acc[...].astype(jnp.bfloat16)

    row = lax.broadcasted_iota(jnp.int32, (8, 128), 0)

    def total_gradient(k, sq):
        for j in range(len(ZOFF)):
            g_copy(k, j).wait_recv()
        t = grad_ref[k]
        for j in range(len(ZOFF)):
            t = t + gr[k, j].astype(jnp.float32)
        grad_ref[k] = t
        return sq + jnp.where(row == k, jnp.sum(t * t), 0.0)

    sqs[...] = lax.fori_loop(0, NK, total_gradient, jnp.zeros((8, 128), jnp.float32))

    def q_copy(j):
        return remote(sqs, sqr.at[x], q_s.at[j], q_r.at[j], at_x(XOFF[j])[1])

    sqr[x] = sqs[...]
    for j in range(len(XOFF)):
        q_copy(j).start()
    for j in range(len(XOFF)):
        q_copy(j).wait_recv()
    squares = sqr[0] + sqr[1] + sqr[2] + sqr[3]

    def y_copy(j):
        return remote(ts, ty.at[me], y_s.at[j], y_r.at[j], at_yc(*EX[j])[1])

    ts[...] = jnp.broadcast_to(jnp.sum(squares, axis=0, keepdims=True), (8, 128))
    ty[me] = ts[...]
    for j in range(len(EX)):
        y_copy(j).start()
    for j in range(len(EX)):
        y_copy(j).wait_recv()

    def z_copy(j):
        return remote(us, tz.at[z], z_s.at[j], z_r.at[j], at_z(ZOFF[j])[1])

    us[...] = jnp.sum(ty[...], axis=0)
    tz[z] = us[...]
    for j in range(len(ZOFF)):
        z_copy(j).start()
    for j in range(len(ZOFF)):
        z_copy(j).wait_recv()
    st_ref[...] = jnp.where(row == NK, jnp.sum(tz[...], axis=0), squares)

    def done(k, carry):
        for j in range(len(EX)):
            ex_copy(k, j).wait_send()
            lora_copy(k, j).wait_send()
        for j in range(len(ZOFF)):
            g_copy(k, j).wait_send()
        for j in range(len(XOFF)):
            base_copy(k, j).wait_send()
            c_copy(k, j).wait_send()
        return carry

    lax.fori_loop(0, NK, done, 0)
    for k in range(NK):
        for s in range(4):
            for up in ag_ways(k, s):
                ag_copy(k, s, up).wait_send()
    for j in range(len(XOFF)):
        q_copy(j).wait_send()
    for j in range(len(EX)):
        y_copy(j).wait_send()
    for j in range(len(ZOFF)):
        z_copy(j).wait_send()


def local(inputs, cotangent, base_weight, adapter_ids, adapters, first_moment, second_moment):
    tok, fw = inputs.shape
    chosen = adapter_ids[:, 0]
    counter = jnp.arange(tok, dtype=jnp.int32)
    matches = (chosen[:, None] == chosen[None, :]) & (counter[None, :] < counter[:, None])
    rank = jnp.sum(matches.astype(jnp.int32), axis=1)
    k = chosen % NK
    core = chosen // NK % NC
    zz = chosen // (NK * NC) % NZ
    yy = chosen // (NK * NC * NZ)
    pos = ((k * GROUP + yy * NC + core) * MOST + rank) * NZ + zz
    bf, f32 = jnp.bfloat16, jnp.float32
    dma = pltpu.SemaphoreType.DMA
    vm, hbm = pl.BlockSpec(memory_space=pltpu.VMEM), pl.BlockSpec(memory_space=pl.ANY)
    out, gradients, stats = pl.pallas_call(
        kernel,
        out_shape=(
            jax.ShapeDtypeStruct((tok, fw), bf),
            jax.ShapeDtypeStruct((NK, 2, R, fw), f32),
            jax.ShapeDtypeStruct((8, 128), f32),
        ),
        in_specs=[vm, vm, hbm, hbm, hbm, vm],
        out_specs=(vm, vm, vm),
        scratch_shapes=[
            pltpu.VMEM((tok, 2 * fw), bf),
            pltpu.VMEM(base_weight.shape, bf),
            pltpu.VMEM((NK, GROUP, CHUNK, 2 * fw), bf),
            pltpu.VMEM((NK, GROUP, CHUNK, 2 * fw), bf),
            pltpu.VMEM((NK, NZ, 2, R, fw), bf),
            pltpu.VMEM((NK, 3, tok // NK, fw), bf),
            pltpu.VMEM((NK, 3, tok // NK, fw), bf),
            pltpu.VMEM((tok, fw), f32),
            pltpu.VMEM((NK, 2, GROUP * MOST, NZ * R), f32),
            pltpu.VMEM((NK, NX, 2, GROUP * MOST, NZ * R), f32),
            pltpu.VMEM((NK, GROUP, CHUNK, fw), bf),
            pltpu.VMEM((NK, GROUP, CHUNK, fw), bf),
            pltpu.VMEM((NK, NZ, 2, R, fw), bf),
            pltpu.VMEM((NK, NZ - 1, 2, R, fw), bf),
            pltpu.VMEM((NZ, 2, R, fw), f32),
            pltpu.VMEM((8, 128), f32),
            pltpu.VMEM((NX, 8, 128), f32),
            pltpu.VMEM((8, 128), f32),
            pltpu.VMEM((GROUP, 8, 128), f32),
            pltpu.VMEM((8, 128), f32),
            pltpu.VMEM((NZ, 8, 128), f32),
            dma((3,)),
            dma((NK, 7)), dma((NK, 7)),
            dma((NK, 8)), dma((NK, 8)),
            dma((NK, 3)), dma((NK, 3)),
            dma((NK, 3)), dma((NK, 3)),
            dma((NK, 7)), dma((NK, 7)),
            dma((NK, 7)), dma((NK, 7)),
            dma((3,)), dma((3,)),
            dma((7,)), dma((7,)),
            dma((7,)), dma((7,)),
        ],
        compiler_params=pltpu.CompilerParams(
            collective_id=0, has_side_effects=True, vmem_limit_bytes=60 * 1024 * 1024
        ),
    )(pos[None, :], pos[:, None], inputs, cotangent, base_weight, adapters)
    new_adapters, new_first, new_second = adam_update(
        adapters, first_moment, second_moment, gradients, stats[:NK, 0]
    )
    return (out, new_adapters, new_first, new_second, jnp.sqrt(stats[NK, 0]))


def solution(mesh):
    in_specs = (
        P("aa", "ba"),
        P("aa", "ba"),
        P(None, "ba"),
        P("aa", None),
        P("aa", None, None, "ba"),
        P("aa", None, None, "ba"),
        P("aa", None, None, "ba"),
    )
    out_specs = (
        P("aa", "ba"),
        P("aa", None, None, "ba"),
        P("aa", None, None, "ba"),
        P("aa", None, None, "ba"),
        P(),
    )
    return jax.shard_map(local, mesh=mesh, in_specs=in_specs, out_specs=out_specs, check_vma=False)
```

time: 246 us -> 110 us (0.45)
  blocking collectives: 117 us -> 0 us
  Pallas kernels: 0 us -> 94.7 us
  waiting for transfers between devices: 46.6 us -> 0 us
  local copies, waits for them, and re-layouts: 26.6 us -> 4.54 us
  matrix products: 17.9 us -> 0 us
  between operations: 16 us -> 2.53 us
  starting transfers between devices: 12.8 us -> 0 us
    all_to_all x3 -> x0, blocking collectives: 117 us -> none  [the longest x1 97.6 us: sent_together(): lax.all_to_all(both, axis, split_axis=split_dim, concat_axis=concat_dim,...]
    pallas_call x0 -> x1, Pallas kernels: none -> 94.7 us  [local(): pl.pallas_call(kernel, out_shape=(jax.ShapeDtypeStruct((tok, fw), bf), ja...]
    all_to_all x2 -> x0, waiting for transfers between devices: 46.5 us -> none  [the longest x1 40.3 us: local(): lax.all_to_all(adapter_rows.reshape(holding_rows, feature_width), 'aa', s...]
    dot_general x6 -> x0, matrix products: 17.9 us -> none  [the longest x1 10.1 us: local(): lax.dot_general(cotangent, base_weight, (((1,), (1,)), ((), ())), preferr...]
    all_to_all x2 -> x0, starting transfers between devices: 12.8 us -> none  [the longest x1 7.98 us: copy_for_each(): return lax.all_to_all(copies, axis, split_axis=0, concat_axis=0, tiled=True)]
    scatter x2 -> x0, local copies, waits for them, and re-layouts: 8.33 us -> none  [local(): jnp.zeros((holding_rows, feature_width), jnp.bfloat16).at[token_position]]
    reshape x4 -> x0, local copies, waits for them, and re-layouts: 6.36 us -> none  [the longest x1 4.21 us: local(): recv_cotangent = recv_cotangent.reshape(grid_shape)]
    add x0 -> x2, other arithmetic: none -> 2.72 us  [local(): pos = ((k * GROUP + yy * NC + core) * MOST + rank) * NZ + zz]
  transfers between devices with their start and end apart: 3 -> 0, of which waited for: 2 -> 0; matrix products, arithmetic and copies ran while one was open for 16% -> 0% of each run, Pallas kernels for 0% -> 0%
where the time goes in v1:
time: 110 us; the launch traced here: 109 us
  Pallas kernels  94.7 us (86%)
  other arithmetic  7.59 us (7%)
  local copies, waits for them, and re-layouts  4.54 us (4%)
  between operations  2.53 us (2%)
    pallas_call x1, Pallas kernels, local(): pl.pallas_call(kernel, out_shape=(jax.ShapeDtypeStruct((tok, fw), bf), ja...  94.7 us
    unnamed x8, local copies, waits for them, and re-layouts  3.01 us
    add x2, other arithmetic, local(): pos = ((k * GROUP + yy * NC + core) * MOST + rank) * NZ + zz  2.72 us
    sub x1, other arithmetic, adam_update(): return (adapters - learn_rate * update, new_first, new_second)  2.34 us

profile of v1, /device:TPU:1, one launch (start us, length us, event | category | flops | bytes accessed | tf_op | source)
XLA Modules:
  0.0 109.3 jit_solution(14537448752804121569)
XLA Ops:
  0.6 0.0 copy-start
  0.6 0.0 copy-start.1
  0.7 0.0 copy-start.2
  0.7 1.0 convert_reduce_fusion
  1.7 1.3 %fusion.20.posr = s32[1,512]{1,0:T(1,128)} fusion(s32[1,512]{1,0:T(1,128)S(1)} %bitcast.25, s32[512,1]{0,1:T(1,128)} %param.10), kind=kLoop, calls=%fused_computation.60 | loop fusion | flops 35328 | bytes 6144 | tf_op jit(solution)/shard_map/add | solution.py:332
  3.0 0.7 broadcast_compare_fusion
  3.7 0.2 copy.39
  3.9 0.1 copy.44
  4.1 0.8 copy.36
  4.9 1.4 %fusion.8.posc = s32[512,1]{1,0:T(8,128)} fusion(s32[512,1]{1,0:T(8,128)S(1)} %copy.44, pred[512,1]{1,0:T(8,128)(4,1)S(1)} %copy.39, s32[512,1]{1,0:T(8,128)S(1)} %copy.36), kind=kLoop, calls=%fused_computation.30 | loop fusion | flops 34816 | bytes 6656 | tf_op jit(solution)/shard_map/add | solution.py:332
  6.3 94.7 %shard_map.110 = (bf16[512,896]{1,0:T(8,128)(2,1)}, f32[4,2,16,896]{3,2,1,0:T(8,128)}, f32[8,128]{1,0:T(8,128)}) custom-call(s32[1,512]{1,0:T(1,128)} %fusion.20.posr, s32[512,1]{1,0:T(8,128)} %fusion.8.posc, bf16[512,896]{1,0:T(8,128)(2,1)} %x_hbm.1, bf16[512,896]{1,0:T(8,128)(2,1)} %g_hbm.1, bf16[3584,896]{1,0:T(8,128)(2,1)} %w_hbm.1, f32[4,2,16,896]{3,2,1,0:T(8,128)} %adf.1), custom_call_target="tpu_custom_call" | custom-call | tf_op jit(solution)/shard_map/pallas_call | solution.py:336
  101.0 1.2 %slice.7 = f32[1,1]{1,0:T(1,128)} slice(f32[8,128]{1,0:T(8,128)} %get-tuple-element.10), slice={[4:5], [0:1]} | slice | bytes 8 | tf_op jit(solution)/shard_map/slice | solution.py:385
  102.9 0.8 fusion.26
  103.7 0.0 copy-done
  103.7 0.0 copy-done.1
  103.7 0.0 copy-done.2
  103.7 2.3 %multiply_subtract_fusion = (f32[4,2,16,896]{3,2,1,0:T(8,128)}, f32[4,2,16,896]{3,2,1,0:T(8,128)}, f32[4,2,16,896]{3,2,1,0:T(8,128)}) fusion(f32[4,2,16,896]{3,2,1,0:T(8,128)S(1)} %copy-done, f32[4,2,16,896]{3,2,1,0:T(8,128)} %get-tuple-element.9, f32[4]{0:T(128)S(1)} %fusion.26, f32[4,2,16,896]{3,2,1,0:T(8,128)S(1)} %copy-done.1, ...), kind=kLoop, calls=%fused_computation.5 | loop fusion | flops 1490944 | bytes 3211280 | tf_op jit(solution)/shard_map/sub | solution.py:39
  106.0 2.2 %copy.49 = bf16[512,896]{1,0:T(8,128)(2,1)} copy(bf16[512,896]{1,0:T(8,128)(2,1)} %get-tuple-element.19) | data formatting | bytes 1835008
Async XLA Ops:
  0.6 103.0 %copy-start = (f32[4,2,16,896]{3,2,1,0:T(8,128)S(1)}, f32[4,2,16,896]{3,2,1,0:T(8,128)}, u32[]{:S(2)}) copy-start(f32[4,2,16,896]{3,2,1,0:T(8,128)} %adf.1) | copy-start | bytes 1376260
  0.6 103.0 %copy-start.1 = (f32[4,2,16,896]{3,2,1,0:T(8,128)S(1)}, f32[4,2,16,896]{3,2,1,0:T(8,128)}, u32[]{:S(2)}) copy-start(f32[4,2,16,896]{3,2,1,0:T(8,128)} %param.13) | copy-start | bytes 1376260
  0.7 103.0 %copy-start.2 = (f32[4,2,16,896]{3,2,1,0:T(8,128)S(1)}, f32[4,2,16,896]{3,2,1,0:T(8,128)}, u32[]{:S(2)}) copy-start(f32[4,2,16,896]{3,2,1,0:T(8,128)} %param.12) | copy-start | bytes 1376260

commit v2 on v1

v2 whole, which is shorter than its diff:
```python
import math

import jax
import jax.numpy as jnp
from jax import lax
from jax.experimental import pallas as pl
from jax.experimental.pallas import tpu as pltpu
from jax.sharding import PartitionSpec as P

MODEL_WIDTH = 3584
R = 16
NY, NZ, NC, NX = 4, 8, 2, 4
NK = 4
MOST = 4
GROUP = NY * NC
CHUNK = NZ * MOST
MESH = pl.DeviceIdType.MESH

adapter_scale = 2.0
beta_first = 0.9
beta_second = 0.999
adam_eps = 1e-08
learn_rate = 0.01
bias_first = 1.0 - math.exp(1000.0 * math.log(beta_first))
bias_second = 1.0 - math.exp(1000.0 * math.log(beta_second))

EX = ((2, 0), (2, 1), (1, 0), (3, 0), (1, 1), (3, 1), (0, 1))
ZOFF = (4, 3, 5, 2, 6, 1, 7)
XOFF = (2, 1, 3)
f32, bf16, i32 = jnp.float32, jnp.bfloat16, jnp.int32


def nt(a, b):
    return lax.dot_general(a, b, (((1,), (1,)), ((), ())), preferred_element_type=f32)


def nn(a, b):
    return jnp.dot(a, b, preferred_element_type=f32)


def kernel(
    ids, x_hbm, g_hbm, w_hbm, ad_hbm,
    out_hbm, grad_hbm, st_ref,
    adf, posr, posc, xg, w, snd, rcv, adb, bs, br, acc, cs, cr, ls, lr, gs, gf, hs, hr, hq, gr, gown, obf,
    sqs, sqr, ts, ty, us, tz,
    lsem, osem, ex_s, ex_r, ag_s, ag_r, b_s, b_r, c_s, c_r, l_s, l_r, g_s, g_r, q_s, q_r, y_s, y_r, z_s, z_r,
):
    a = lax.axis_index("aa")
    x = lax.axis_index("ba")
    y, z, c = a // (NZ * NC), (a // NC) % NZ, a % NC
    me = y * NC + c
    tok, fw = x_hbm.shape
    nrow = GROUP * CHUNK
    quarter = tok // NK

    def at_yc(dy, dc):
        yy, cc = (y + dy) % NY, (c + dc) % NC
        return yy * NC + cc, ((yy * NZ + z) * NC + cc, x)

    def at_z(dz):
        zz = (z + dz + NZ) % NZ
        return zz, ((y * NZ + zz) * NC + c, x)

    def at_x(dx):
        xx = (x + dx) % NX
        return xx, (a, xx)

    barrier = pltpu.get_barrier_semaphore()
    for dz in ZOFF:
        pl.semaphore_signal(barrier, inc=1, device_id=at_z(dz)[1], device_id_type=MESH)
    for dy, dc in EX:
        pl.semaphore_signal(barrier, inc=1, device_id=at_yc(dy, dc)[1], device_id_type=MESH)
    for dx in XOFF:
        pl.semaphore_signal(barrier, inc=1, device_id=at_x(dx)[1], device_id_type=MESH)

    loads = [
        pltpu.make_async_copy(ad_hbm, adf, lsem.at[0]),
        pltpu.make_async_copy(x_hbm, xg.at[:, 0:fw], lsem.at[1]),
        pltpu.make_async_copy(g_hbm, xg.at[:, fw : 2 * fw], lsem.at[2]),
        pltpu.make_async_copy(w_hbm, w, lsem.at[3]),
    ]
    for cp in loads:
        cp.start()

    def remote(src, dst, ssem, rsem, dev):
        return pltpu.make_async_remote_copy(
            src_ref=src, dst_ref=dst, send_sem=ssem, recv_sem=rsem, device_id=dev, device_id_type=MESH
        )

    def ex_copy(k, j):
        d, dev = at_yc(*EX[j])
        return remote(snd.at[k, d], rcv.at[k, me], ex_s.at[k, j], ex_r.at[k, j], dev)

    def lora_copy(k, j):
        d, dev = at_yc(*EX[j])
        return remote(ls.at[k, d], lr.at[k, me], l_s.at[k, j], l_r.at[k, j], dev)

    def ag_copy(k, s, up):
        o, i = at_z(-s if up else s)[0], s if up else 4 + s
        return remote(adb.at[k, o], adb.at[k, o], ag_s.at[k, i], ag_r.at[k, i], at_z(1 if up else -1)[1])

    def g_copy(k, j):
        side = 1 if j % 2 == 0 else -1
        if j < 2:
            src, dst, to = gs.at[k, at_z(side)[0]], gr.at[k, j], side
        elif j < 4:
            src, dst, to = gs.at[k, at_z(3 * side)[0]], hr.at[k, j - 2], side
        elif j < 6:
            src, dst, to = gs.at[k, at_z(4)[0], j - 4], hq.at[k, j - 4], 2 * side
        else:
            src, dst, to = hs.at[k, j - 6], gr.at[k, j - 4], 2 * side
        return remote(src, dst, g_s.at[k, j], g_r.at[k, j], at_z(to)[1])

    def base_copy(q, j):
        here = pl.ds(q * quarter, quarter)
        return remote(bs.at[j, here, :], br.at[j, here, :], b_s.at[q, j], b_r.at[q, j], at_x(XOFF[j])[1])

    def c_copy(k, j):
        return remote(cs.at[k], cr.at[k, x], c_s.at[k, j], c_r.at[k, j], at_x(XOFF[j])[1])

    def q_copy(j):
        return remote(sqs, sqr.at[x], q_s.at[j], q_r.at[j], at_x(XOFF[j])[1])

    def y_copy(j):
        return remote(ts, ty.at[me], y_s.at[j], y_r.at[j], at_yc(*EX[j])[1])

    def z_copy(j):
        return remote(us, tz.at[z], z_s.at[j], z_r.at[j], at_z(ZOFF[j])[1])

    def positions():
        row = ids[...]
        col = jnp.broadcast_to(row, (128, tok)).T[:, 0:1]
        before = lax.broadcasted_iota(i32, (tok, 1), 0) < lax.broadcasted_iota(i32, (1, tok), 1)
        rank = jnp.sum(jnp.where((col == row) & before, 1, 0), axis=0, keepdims=True)
        k, core = row & (NK - 1), (row >> 2) & (NC - 1)
        zz, yy = (row >> 3) & (NZ - 1), row >> 6
        pos = ((k * GROUP + yy * NC + core) * MOST + rank) * NZ + zz
        posr[...] = pos
        posc[...] = jnp.broadcast_to(pos, (128, tok)).T

    def gather(k):
        rows = lax.broadcasted_iota(i32, (nrow, 1), 0) + k * nrow
        hot = jnp.where(rows == posr[...], 1.0, 0.0).astype(bf16)
        snd[k] = nn(hot, xg[...]).astype(bf16).reshape(GROUP, CHUNK, 2 * fw)
        rcv[k, me] = snd[k, me]

    def send_tokens(k):
        for j in range(len(EX)):
            ex_copy(k, j).start()

    def frozen_of(dx):
        xx = at_x(dx)[0]
        return nt(xg[:, fw : 2 * fw], w[pl.ds(pl.multiple_of(xx * fw, fw), fw), :])

    def frozen_for(j):
        bs[j] = frozen_of(XOFF[j]).astype(bf16)

    def ag_ways(k, s):
        return [up for up in (True, False) if s < 3 or up == (k % 2 == 0)]

    def ag_pass(k, s):
        for up in ag_ways(k, s):
            if s > 0:
                ag_copy(k, s - 1, up).wait_recv()
            ag_copy(k, s, up).start()

    def ag_end(k):
        for up in (True, False):
            ag_copy(k, 3 if up in ag_ways(k, 3) else 2, up).wait_recv()

    lane = lax.broadcasted_iota(i32, (1, NZ, NZ * R), 2) // R
    sub = lax.broadcasted_iota(i32, (1, NZ, NZ * R), 1)
    mine = lane == sub

    def rows_of(k, first):
        return rcv[k, :, :, first : first + fw].reshape(nrow, fw)

    def project(k):
        pulled = nt(rows_of(k, fw), adb[k, :, 1].reshape(NZ * R, fw)).reshape(GROUP * MOST, NZ, NZ * R)
        projected = nt(rows_of(k, 0), adb[k, :, 0].reshape(NZ * R, fw)).reshape(GROUP * MOST, NZ, NZ * R)
        cs[k, 0] = jnp.sum(jnp.where(mine, pulled, 0.0), axis=1)
        cs[k, 1] = jnp.sum(jnp.where(mine, projected, 0.0), axis=1)
        cr[k, x] = cs[k]
        for j in range(len(XOFF)):
            c_copy(k, j).start()

    def gradients(k):
        low = (cr[k, 0] + cr[k, 1] + cr[k, 2] + cr[k, 3]).astype(bf16).astype(f32)
        pull = jnp.where(mine, low[0][:, None, :], 0.0).reshape(nrow, NZ * R)
        proj = jnp.where(mine, low[1][:, None, :], 0.0).reshape(nrow, NZ * R)
        for i, (side, first) in enumerate(((pull, 0), (proj, fw))):
            grad = (adapter_scale * nn(side.T.astype(bf16), rows_of(k, first))).reshape(NZ, R, fw)
            gf[:, i] = grad
            gs[k, :, i] = grad.astype(bf16)
        for j in (2, 3, 4, 5, 0, 1):
            g_copy(k, j).start()
        gown[k] = gf[z]
        lora = adapter_scale * nn(pull.astype(bf16), adb[k, :, 0].reshape(NZ * R, fw))
        ls[k] = lora.astype(bf16).reshape(GROUP, CHUNK, fw)
        for j in range(len(EX)):
            lora_copy(k, j).start()
        lr[k, me] = ls[k, me]

    def hub(k):
        for side in range(2):
            g_copy(k, 2 + side).wait_recv()
            g_copy(k, 4 + side).wait_recv()
            sign = 1 if side == 0 else -1
            for i in range(2):
                t = gf[at_z(2 * sign)[0], i] + hr[k, side, i].astype(f32)
                if i == side:
                    t = t + hq[k, side].astype(f32)
                hs[k, side, i] = t.astype(bf16)
            g_copy(k, 6 + side).start()

    def unslot(k):
        cols = lax.broadcasted_iota(i32, (1, nrow), 1) + k * nrow
        hot = jnp.where(posc[:, 0:1] == cols, 1.0, 0.0).astype(bf16)
        acc[...] += nn(hot, lr[k].reshape(nrow, fw))

    def total_gradient(k):
        for j in (0, 1, 6, 7):
            g_copy(k, j).wait_recv()
        t = gown[k]
        for j in range(4):
            t = t + gr[k, j].astype(f32)
        gown[k] = t
        return jnp.sum(t * t)

    for k in range(NK):
        if k == 0:
            loads[0].wait()
        adb[k, z] = adf[k].astype(bf16)
    positions()
    loads[1].wait()
    loads[2].wait()
    for k in range(NK):
        gather(k)
    loads[3].wait()
    frozen_for(0)
    pl.semaphore_wait(barrier, len(EX) + len(ZOFF) + len(XOFF))

    ag_pass(0, 0)
    send_tokens(0)
    base_copy(0, 0).start()
    ag_pass(1, 0)
    for k in range(1, NK):
        send_tokens(k)
    frozen_for(1)
    base_copy(0, 1).start()
    ag_pass(0, 1)
    ag_pass(2, 0)
    frozen_for(2)
    base_copy(0, 2).start()
    base_copy(1, 0).start()
    ag_pass(1, 1)
    ag_pass(0, 2)
    ag_pass(3, 0)
    ag_pass(2, 1)
    ag_pass(1, 2)
    ag_pass(0, 3)
    acc[...] = frozen_of(0)
    ag_pass(3, 1)
    ag_pass(2, 2)
    ag_pass(1, 3)
    ag_end(0)

    later = ([(1, 1), (1, 2)], [(2, 0), (2, 1), (2, 2)], [(3, 0)], [(3, 1), (3, 2)])
    for k in range(NK):
        if k > 0:
            ag_end(k)
        for j in range(len(EX)):
            ex_copy(k, j).wait_recv()
        project(k)
        for q, j in later[k]:
            base_copy(q, j).start()
        if k == 0:
            ag_pass(3, 2)
            ag_pass(2, 3)
            ag_pass(3, 3)
        else:
            hub(k - 1)
        for j in range(len(XOFF)):
            c_copy(k, j).wait_recv()
        gradients(k)

    def frozen(q):
        here = pl.ds(q * quarter, quarter)
        for j in range(len(XOFF)):
            base_copy(q, j).wait_recv()
        t = acc[here, :]
        for j in range(len(XOFF)):
            t = t + br[j, here, :].astype(f32)
        acc[here, :] = t

    def lora_wait(k):
        for j in range(len(EX)):
            lora_copy(k, j).wait_recv()

    frozen(0)
    frozen(1)
    lora_wait(0)
    unslot(0)
    hub(NK - 1)
    frozen(2)
    lora_wait(1)
    unslot(1)
    row = lax.broadcasted_iota(i32, (8, 128), 0)
    sq = jnp.zeros((8, 128), f32)
    for k in range(NK):
        sq = sq + jnp.where(row == k, total_gradient(k), 0.0)
    sqs[...] = sq
    for j in range(len(XOFF)):
        q_copy(j).start()
    sqr[x] = sq
    grad_out = pltpu.make_async_copy(gown, grad_hbm, osem.at[0])
    grad_out.start()
    frozen(3)
    lora_wait(2)
    unslot(2)
    for j in range(len(XOFF)):
        q_copy(j).wait_recv()
    squares = sqr[0] + sqr[1] + sqr[2] + sqr[3]
    ts[...] = jnp.broadcast_to(jnp.sum(squares, axis=0, keepdims=True), (8, 128))
    for j in range(len(EX)):
        y_copy(j).start()
    ty[me] = ts[...]
    for j in range(len(EX)):
        y_copy(j).wait_recv()
    us[...] = jnp.sum(ty[...], axis=0)
    for j in range(len(ZOFF)):
        z_copy(j).start()
    tz[z] = us[...]
    lora_wait(3)
    unslot(3)
    obf[...] = acc[...].astype(bf16)
    out_copy = pltpu.make_async_copy(obf, out_hbm, osem.at[1])
    out_copy.start()
    for k in range(NK):
        for j in range(len(EX)):
            ex_copy(k, j).wait_send()
            lora_copy(k, j).wait_send()
        for j in range(8):
            g_copy(k, j).wait_send()
        for j in range(len(XOFF)):
            base_copy(k, j).wait_send()
            c_copy(k, j).wait_send()
        for s in range(4):
            for up in ag_ways(k, s):
                ag_copy(k, s, up).wait_send()
    for j in range(len(XOFF)):
        q_copy(j).wait_send()
    for j in range(len(EX)):
        y_copy(j).wait_send()
    for j in range(len(ZOFF)):
        z_copy(j).wait_recv()
    st_ref[...] = jnp.where(row == NK, jnp.sum(tz[...], axis=0), squares)
    for j in range(len(ZOFF)):
        z_copy(j).wait_send()
    grad_out.wait()
    out_copy.wait()


def finish(out_ref, grad_ref, st_ref, ad_ref, m_ref, v_ref, o_ref, na_ref, nf_ref, ns_ref, norm_ref):
    clip_limit = math.sqrt(2.0 * R * MODEL_WIDTH)
    o_ref[...] = out_ref[...]
    for k in range(NK):
        factor = clip_limit / jnp.maximum(jnp.sqrt(st_ref[k : k + 1, 0:1]), clip_limit)
        clipped = grad_ref[k] * factor
        new_first = beta_first * m_ref[k] + (1.0 - beta_first) * clipped
        new_second = beta_second * v_ref[k] + (1.0 - beta_second) * clipped * clipped
        update = new_first / bias_first / (jnp.sqrt(new_second / bias_second) + adam_eps)
        na_ref[k] = ad_ref[k] - learn_rate * update
        nf_ref[k] = new_first
        ns_ref[k] = new_second
    norm_ref[...] = jnp.sqrt(st_ref[NK : NK + 1, 0:1])


def local(inputs, cotangent, base_weight, adapter_ids, adapters, first_moment, second_moment):
    tok, fw = inputs.shape
    dma = pltpu.SemaphoreType.DMA
    vm, hbm = pl.BlockSpec(memory_space=pltpu.VMEM), pl.BlockSpec(memory_space=pl.ANY)
    own = (NK, 2, R, fw)
    out, grads, stats = pl.pallas_call(
        kernel,
        out_shape=(
            jax.ShapeDtypeStruct((tok, fw), bf16),
            jax.ShapeDtypeStruct(own, f32),
            jax.ShapeDtypeStruct((8, 128), f32),
        ),
        in_specs=[vm, hbm, hbm, hbm, hbm],
        out_specs=(hbm, hbm, vm),
        scratch_shapes=[
            pltpu.VMEM(own, f32),
            pltpu.VMEM((1, tok), i32),
            pltpu.VMEM((tok, 128), i32),
            pltpu.VMEM((tok, 2 * fw), bf16),
            pltpu.VMEM(base_weight.shape, bf16),
            pltpu.VMEM((NK, GROUP, CHUNK, 2 * fw), bf16),
            pltpu.VMEM((NK, GROUP, CHUNK, 2 * fw), bf16),
            pltpu.VMEM((NK, NZ, 2, R, fw), bf16),
            pltpu.VMEM((3, tok, fw), bf16),
            pltpu.VMEM((3, tok, fw), bf16),
            pltpu.VMEM((tok, fw), f32),
            pltpu.VMEM((NK, 2, GROUP * MOST, NZ * R), f32),
            pltpu.VMEM((NK, NX, 2, GROUP * MOST, NZ * R), f32),
            pltpu.VMEM((NK, GROUP, CHUNK, fw), bf16),
            pltpu.VMEM((NK, GROUP, CHUNK, fw), bf16),
            pltpu.VMEM((NK, NZ, 2, R, fw), bf16),
            pltpu.VMEM((NZ, 2, R, fw), f32),
            pltpu.VMEM((NK, 2, 2, R, fw), bf16),
            pltpu.VMEM((NK, 2, 2, R, fw), bf16),
            pltpu.VMEM((NK, 2, R, fw), bf16),
            pltpu.VMEM((NK, 4, 2, R, fw), bf16),
            pltpu.VMEM(own, f32),
            pltpu.VMEM((tok, fw), bf16),
            pltpu.VMEM((8, 128), f32),
            pltpu.VMEM((NX, 8, 128), f32),
            pltpu.VMEM((8, 128), f32),
            pltpu.VMEM((GROUP, 8, 128), f32),
            pltpu.VMEM((8, 128), f32),
            pltpu.VMEM((NZ, 8, 128), f32),
            dma((4,)), dma((2,)),
            dma((NK, 7)), dma((NK, 7)),
            dma((NK, 8)), dma((NK, 8)),
            dma((NK, 3)), dma((NK, 3)),
            dma((NK, 3)), dma((NK, 3)),
            dma((NK, 7)), dma((NK, 7)),
            dma((NK, 8)), dma((NK, 8)),
            dma((3,)), dma((3,)),
            dma((7,)), dma((7,)),
            dma((7,)), dma((7,)),
        ],
        compiler_params=pltpu.CompilerParams(
            collective_id=0, has_side_effects=True, vmem_limit_bytes=62 * 1024 * 1024
        ),
    )(adapter_ids.reshape(1, tok), inputs, cotangent, base_weight, adapters)
    out, new_adapters, new_first, new_second, norm = pl.pallas_call(
        finish,
        out_shape=(
            jax.ShapeDtypeStruct((tok, fw), bf16),
            jax.ShapeDtypeStruct(own, f32),
            jax.ShapeDtypeStruct(own, f32),
            jax.ShapeDtypeStruct(own, f32),
            jax.ShapeDtypeStruct((1, 1), f32),
        ),
        in_specs=[vm] * 6,
        out_specs=(vm,) * 5,
        compiler_params=pltpu.CompilerParams(vmem_limit_bytes=62 * 1024 * 1024),
    )(out, grads, stats, adapters, first_moment, second_moment)
    return (out, new_adapters, new_first, new_second, norm.reshape(()))


def solution(mesh):
    in_specs = (
        P("aa", "ba"),
        P("aa", "ba"),
        P(None, "ba"),
        P("aa", None),
        P("aa", None, None, "ba"),
        P("aa", None, None, "ba"),
        P("aa", None, None, "ba"),
    )
    out_specs = (
        P("aa", "ba"),
        P("aa", None, None, "ba"),
        P("aa", None, None, "ba"),
        P("aa", None, None, "ba"),
        P(),
    )
    return jax.shard_map(local, mesh=mesh, in_specs=in_specs, out_specs=out_specs, check_vma=False)
```

time: 110 us -> 88.5 us (0.80)
  other arithmetic: 7.59 us -> 0 us
  Pallas kernels: 94.7 us -> 87.7 us
  local copies, waits for them, and re-layouts: 4.54 us -> 0 us
  between operations: 2.53 us -> 0.64 us
    pallas_call x1 -> x2, Pallas kernels: 94.7 us -> 87.7 us  [the longest x1 84.4 us: local(): pl.pallas_call(kernel, out_shape=(jax.ShapeDtypeStruct((tok, fw), bf16),...]
    unnamed x8 -> x0, local copies, waits for them, and re-layouts: 3.01 us -> none
    add x2 -> x0, other arithmetic: 2.72 us -> none  [local(): pos = ((k * GROUP + yy * NC + core) * MOST + rank) * NZ + zz]
    sub x1 -> x0, other arithmetic: 2.34 us -> none  [adam_update(): return (adapters - learn_rate * update, new_first, new_second)]
    slice x1 -> x0, local copies, waits for them, and re-layouts: 1.19 us -> none  [local(): return (out, new_adapters, new_first, new_second, jnp.sqrt(stats[NK, 0]))]
where the time goes in v2:
time: 88.5 us; the launch traced here: 88.3 us
  Pallas kernels  87.7 us (99%)
    pallas_call x1, Pallas kernels, local(): pl.pallas_call(kernel, out_shape=(jax.ShapeDtypeStruct((tok, fw), bf16),...  84.4 us
    pallas_call x1, Pallas kernels, local(): pl.pallas_call(finish, out_shape=(jax.ShapeDtypeStruct((tok, fw), bf16),...  3.31 us

profile of v2, /device:TPU:1, one launch (start us, length us, event | category | flops | bytes accessed | tf_op | source)
XLA Modules:
  0.0 88.3 jit_solution(5239569187513982149)
XLA Ops:
  0.6 84.4 %shard_map.110 = (bf16[512,896]{1,0:T(8,128)(2,1)}, f32[4,2,16,896]{3,2,1,0:T(8,128)}, f32[8,128]{1,0:T(8,128)}) custom-call(s32[1,512]{1,0:T(1,128)} %bitcast.2, bf16[512,896]{1,0:T(8,128)(2,1)} %x_hbm.1, bf16[512,896]{1,0:T(8,128)(2,1)} %g_hbm.1, bf16[3584,896]{1,0:T(8,128)(2,1)} %w_hbm.1, f32[4,2,16,896]{3,2,1,0:T(8,128)} %ad_ref.1), custom_call_target="tpu_custom_call" | custom-call | tf_op jit(solution)/shard_map/pallas_call | solution.py:384
  85.0 3.3 %shard_map.111 = (bf16[512,896]{1,0:T(8,128)(2,1)}, f32[4,2,16,896]{3,2,1,0:T(8,128)}, f32[4,2,16,896]{3,2,1,0:T(8,128)}, f32[4,2,16,896]{3,2,1,0:T(8,128)}, f32[1,1]{1,0:T(1,128)}) custom-call(bf16[512,896]{1,0:T(8,128)(2,1)} %get-tuple-element.13.out_ref, f32[4,2,16,896]{3,2,1,0:T(8,128)} %get-tuple-element.14.grad_ref, ...), custom_call_target="tpu_custom_call" | custom-call | tf_op jit(solution)/shard_map/pallas_call | solution.py:438

commit v3 on v2

--- a/solution.py
+++ b/solution.py
@@ -27,6 +27,7 @@
 EX = ((2, 0), (2, 1), (1, 0), (3, 0), (1, 1), (3, 1), (0, 1))
 ZOFF = (4, 3, 5, 2, 6, 1, 7)
 XOFF = (2, 1, 3)
+ALL = tuple((dy, dc, dx) for dy in (2, 1, 3, 0) for dx in (2, 1, 3, 0) for dc in (1, 0) if (dy, dc, dx) != (0, 0, 0))
 f32, bf16, i32 = jnp.float32, jnp.bfloat16, jnp.int32
 
 
@@ -39,11 +40,11 @@
 
 
 def kernel(
-    ids, x_hbm, g_hbm, w_hbm, ad_hbm,
+    ids_hbm, x_hbm, g_hbm, w_hbm, ad_hbm,
     out_hbm, grad_hbm, st_ref,
-    adf, posr, posc, xg, w, snd, rcv, adb, bs, br, acc, cs, cr, ls, lr, gs, gf, hs, hr, hq, gr, gown, obf,
+    adf, ids, posr, posc, xg, w, snd, rcv, adb, far, via, bs, br, acc, cs, cr, ls, lr, gs, gf, hs, hr, gr, gown, obf,
     sqs, sqr, ts, ty, us, tz,
-    lsem, osem, ex_s, ex_r, ag_s, ag_r, b_s, b_r, c_s, c_r, l_s, l_r, g_s, g_r, q_s, q_r, y_s, y_r, z_s, z_r,
+    lsem, osem, ex_s, ex_r, ag_s, ag_r, f_s, f_r, b_s, b_r, c_s, c_r, l_s, l_r, g_s, g_r, h_r, q_s, q_r, y_s, y_r, z_s, z_r,
 ):
     a = lax.axis_index("aa")
     x = lax.axis_index("ba")
@@ -61,6 +62,10 @@
         zz = (z + dz + NZ) % NZ
         return zz, ((y * NZ + zz) * NC + c, x)
 
+    def at_all(dy, dc, dx):
+        yy, cc = (y + dy) % NY, (c + dc) % NC
+        return (yy * NZ + z) * NC + cc, (x + dx) % NX
+
     def at_x(dx):
         xx = (x + dx) % NX
         return xx, (a, xx)
@@ -68,13 +73,12 @@
     barrier = pltpu.get_barrier_semaphore()
     for dz in ZOFF:
         pl.semaphore_signal(barrier, inc=1, device_id=at_z(dz)[1], device_id_type=MESH)
-    for dy, dc in EX:
-        pl.semaphore_signal(barrier, inc=1, device_id=at_yc(dy, dc)[1], device_id_type=MESH)
-    for dx in XOFF:
-        pl.semaphore_signal(barrier, inc=1, device_id=at_x(dx)[1], device_id_type=MESH)
+    for step in ALL:
+        pl.semaphore_signal(barrier, inc=1, device_id=at_all(*step), device_id_type=MESH)
 
     loads = [
         pltpu.make_async_copy(ad_hbm, adf, lsem.at[0]),
+        pltpu.make_async_copy(ids_hbm, ids, lsem.at[4]),
         pltpu.make_async_copy(x_hbm, xg.at[:, 0:fw], lsem.at[1]),
         pltpu.make_async_copy(g_hbm, xg.at[:, fw : 2 * fw], lsem.at[2]),
         pltpu.make_async_copy(w_hbm, w, lsem.at[3]),
@@ -87,45 +91,55 @@
             src_ref=src, dst_ref=dst, send_sem=ssem, recv_sem=rsem, device_id=dev, device_id_type=MESH
         )
 
+    def arrived(ref, sem):
+        remote(ref, ref, sem, sem, at_x(1)[1]).wait_recv()
+
+    def left(ref, sem):
+        remote(ref, ref, sem, sem, at_x(1)[1]).wait_send()
+
     def ex_copy(k, j):
         d, dev = at_yc(*EX[j])
-        return remote(snd.at[k, d], rcv.at[k, me], ex_s.at[k, j], ex_r.at[k, j], dev)
+        return remote(snd.at[k, d], rcv.at[k, me], ex_s, ex_r.at[k], dev)
 
     def lora_copy(k, j):
         d, dev = at_yc(*EX[j])
-        return remote(ls.at[k, d], lr.at[k, me], l_s.at[k, j], l_r.at[k, j], dev)
+        return remote(ls.at[k, d], lr.at[k, me], l_s, l_r.at[k], dev)
 
     def ag_copy(k, s, up):
         o, i = at_z(-s if up else s)[0], s if up else 4 + s
-        return remote(adb.at[k, o], adb.at[k, o], ag_s.at[k, i], ag_r.at[k, i], at_z(1 if up else -1)[1])
+        return remote(adb.at[k, o], adb.at[k, o], ag_s, ag_r.at[k, i], at_z(1 if up else -1)[1])
 
     def g_copy(k, j):
         side = 1 if j % 2 == 0 else -1
         if j < 2:
-            src, dst, to = gs.at[k, at_z(side)[0]], gr.at[k, j], side
+            src, dst, to, sem = gs.at[k, at_z(side)[0]], gr.at[k, j], side, g_r.at[k]
         elif j < 4:
-            src, dst, to = gs.at[k, at_z(3 * side)[0]], hr.at[k, j - 2], side
+            src, dst, to, sem = gs.at[k, at_z(3 * side)[0]], hr.at[k, j - 2, 0:2], side, h_r.at[k, j - 2]
         elif j < 6:
-            src, dst, to = gs.at[k, at_z(4)[0], j - 4], hq.at[k, j - 4], 2 * side
+            src, dst, to, sem = gs.at[k, at_z(4)[0], j - 4], hr.at[k, j - 4, 2], 2 * side, h_r.at[k, j - 4]
         else:
-            src, dst, to = hs.at[k, j - 6], gr.at[k, j - 4], 2 * side
-        return remote(src, dst, g_s.at[k, j], g_r.at[k, j], at_z(to)[1])
-
-    def base_copy(q, j):
+            src, dst, to, sem = hs.at[k, j - 6], gr.at[k, j - 4], 2 * side, g_r.at[k]
+        return remote(src, dst, g_s, sem, at_z(to)[1])
+
+    def far_copy(j):
+        half = pl.ds(j * (tok // 2), tok // 2)
+        return remote(far.at[half, :], via.at[j], f_s, f_r.at[j], at_x(1 if j == 0 else 3)[1])
+
+    def near_copy(q, j):
         here = pl.ds(q * quarter, quarter)
-        return remote(bs.at[j, here, :], br.at[j, here, :], b_s.at[q, j], b_r.at[q, j], at_x(XOFF[j])[1])
+        return remote(bs.at[j, here, :], br.at[j, here, :], b_s, b_r.at[q], at_x(1 if j == 0 else 3)[1])
 
     def c_copy(k, j):
-        return remote(cs.at[k], cr.at[k, x], c_s.at[k, j], c_r.at[k, j], at_x(XOFF[j])[1])
+        return remote(cs.at[k], cr.at[k, x], c_s, c_r.at[k], at_x(XOFF[j])[1])
 
     def q_copy(j):
-        return remote(sqs, sqr.at[x], q_s.at[j], q_r.at[j], at_x(XOFF[j])[1])
+        return remote(sqs, sqr.at[x], q_s, q_r, at_x(XOFF[j])[1])
 
     def y_copy(j):
-        return remote(ts, ty.at[me], y_s.at[j], y_r.at[j], at_yc(*EX[j])[1])
+        return remote(us, ty.at[x * GROUP + me], y_s, y_r, at_all(*ALL[j]))
 
     def z_copy(j):
-        return remote(us, tz.at[z], z_s.at[j], z_r.at[j], at_z(ZOFF[j])[1])
+        return remote(ts, tz.at[z], z_s, z_r, at_z(ZOFF[j])[1])
 
     def positions():
         row = ids[...]
@@ -148,12 +162,25 @@
         for j in range(len(EX)):
             ex_copy(k, j).start()
 
-    def frozen_of(dx):
+    def frozen_of(dx, here):
         xx = at_x(dx)[0]
-        return nt(xg[:, fw : 2 * fw], w[pl.ds(pl.multiple_of(xx * fw, fw), fw), :])
-
-    def frozen_for(j):
-        bs[j] = frozen_of(XOFF[j]).astype(bf16)
+        return nt(xg[here, fw : 2 * fw], w[pl.ds(pl.multiple_of(xx * fw, fw), fw), :])
+
+    def frozen_far():
+        far[...] = frozen_of(2, slice(None)).astype(bf16)
+        for j in range(2):
+            far_copy(j).start()
+
+    def frozen_near(q):
+        here = pl.ds(q * quarter, quarter)
+        for j in range(2):
+            t = frozen_of(1 if j == 0 else 3, here)
+            if q // 2 == j:
+                if q % 2 == 0:
+                    arrived(via.at[j], f_r.at[j])
+                t = t + via[j, pl.ds((q % 2) * quarter, quarter), :].astype(f32)
+            bs[j, here, :] = t.astype(bf16)
+            near_copy(q, j).start()
 
     def ag_ways(k, s):
         return [up for up in (True, False) if s < 3 or up == (k % 2 == 0)]
@@ -203,13 +230,12 @@
 
     def hub(k):
         for side in range(2):
-            g_copy(k, 2 + side).wait_recv()
-            g_copy(k, 4 + side).wait_recv()
+            arrived(hr.at[k, side], h_r.at[k, side])
             sign = 1 if side == 0 else -1
             for i in range(2):
                 t = gf[at_z(2 * sign)[0], i] + hr[k, side, i].astype(f32)
                 if i == side:
-                    t = t + hq[k, side].astype(f32)
+                    t = t + hr[k, side, 2].astype(f32)
                 hs[k, side, i] = t.astype(bf16)
             g_copy(k, 6 + side).start()
 
@@ -219,83 +245,75 @@
         acc[...] += nn(hot, lr[k].reshape(nrow, fw))
 
     def total_gradient(k):
-        for j in (0, 1, 6, 7):
-            g_copy(k, j).wait_recv()
+        arrived(gr.at[k], g_r.at[k])
         t = gown[k]
         for j in range(4):
             t = t + gr[k, j].astype(f32)
         gown[k] = t
         return jnp.sum(t * t)
 
-    for k in range(NK):
-        if k == 0:
-            loads[0].wait()
+    loads[0].wait()
+    for k in range(2):
         adb[k, z] = adf[k].astype(bf16)
+    for cp in loads[1:4]:
+        cp.wait()
     positions()
-    loads[1].wait()
-    loads[2].wait()
-    for k in range(NK):
-        gather(k)
-    loads[3].wait()
-    frozen_for(0)
-    pl.semaphore_wait(barrier, len(EX) + len(ZOFF) + len(XOFF))
-
+    gather(0)
+    pl.semaphore_wait(barrier, len(ZOFF) + len(ALL))
     ag_pass(0, 0)
     send_tokens(0)
-    base_copy(0, 0).start()
     ag_pass(1, 0)
-    for k in range(1, NK):
-        send_tokens(k)
-    frozen_for(1)
-    base_copy(0, 1).start()
+    for k in range(2, NK):
+        adb[k, z] = adf[k].astype(bf16)
+    loads[4].wait()
+    frozen_far()
     ag_pass(0, 1)
     ag_pass(2, 0)
-    frozen_for(2)
-    base_copy(0, 2).start()
-    base_copy(1, 0).start()
+    gather(1)
+    send_tokens(1)
     ag_pass(1, 1)
+    ag_pass(3, 0)
+    gather(2)
+    send_tokens(2)
     ag_pass(0, 2)
-    ag_pass(3, 0)
     ag_pass(2, 1)
+    gather(3)
+    send_tokens(3)
     ag_pass(1, 2)
+    ag_pass(3, 1)
+    acc[...] = frozen_of(0, slice(None))
     ag_pass(0, 3)
-    acc[...] = frozen_of(0)
-    ag_pass(3, 1)
     ag_pass(2, 2)
     ag_pass(1, 3)
     ag_end(0)
 
-    later = ([(1, 1), (1, 2)], [(2, 0), (2, 1), (2, 2)], [(3, 0)], [(3, 1), (3, 2)])
     for k in range(NK):
+        if k == NK - 1:
+            hub(k - 1)
         if k > 0:
             ag_end(k)
-        for j in range(len(EX)):
-            ex_copy(k, j).wait_recv()
+        arrived(rcv.at[k, 0 : GROUP - 1], ex_r.at[k])
         project(k)
-        for q, j in later[k]:
-            base_copy(q, j).start()
         if k == 0:
             ag_pass(3, 2)
             ag_pass(2, 3)
             ag_pass(3, 3)
-        else:
+        elif k < NK - 1:
             hub(k - 1)
-        for j in range(len(XOFF)):
-            c_copy(k, j).wait_recv()
+        arrived(cr.at[k, 0 : NX - 1], c_r.at[k])
         gradients(k)
+        frozen_near(k)
 
     def frozen(q):
         here = pl.ds(q * quarter, quarter)
-        for j in range(len(XOFF)):
-            base_copy(q, j).wait_recv()
+        arrived(br.at[:, here, :], b_r.at[q])
         t = acc[here, :]
-        for j in range(len(XOFF)):
+        for j in range(2):
             t = t + br[j, here, :].astype(f32)
         acc[here, :] = t
 
     def lora_wait(k):
-        for j in range(len(EX)):
-            lora_copy(k, j).wait_recv()
+        arrived(lr.at[k, 0 : GROUP - 1], l_r.at[k])
 
     frozen(0)
     frozen(1)
@@ -310,54 +328,43 @@
     for k in range(NK):
         sq = sq + jnp.where(row == k, total_gradient(k), 0.0)
     sqs[...] = sq
+    ts[...] = jnp.sum(sq, axis=0, keepdims=True)
+    for j in range(len(ZOFF)):
+        z_copy(j).start()
     for j in range(len(XOFF)):
         q_copy(j).start()
     sqr[x] = sq
+    tz[z] = ts[...]
     grad_out = pltpu.make_async_copy(gown, grad_hbm, osem.at[0])
     grad_out.start()
     frozen(3)
+    arrived(tz.at[0 : NZ - 1], z_r)
+    us[...] = jnp.sum(tz[...], axis=0)
+    for j in range(len(ALL)):
+        y_copy(j).start()
+    ty[x * GROUP + me] = us[...]
     lora_wait(2)
     unslot(2)
-    for j in range(len(XOFF)):
-        q_copy(j).wait_recv()
+    arrived(sqr.at[0 : NX - 1], q_r)
     squares = sqr[0] + sqr[1] + sqr[2] + sqr[3]
-    ts[...] = jnp.broadcast_to(jnp.sum(squares, axis=0, keepdims=True), (8, 128))
-    for j in range(len(EX)):
-        y_copy(j).start()
-    ty[me] = ts[...]
-    for j in range(len(EX)):
-        y_copy(j).wait_recv()
-    us[...] = jnp.sum(ty[...], axis=0)
-    for j in range(len(ZOFF)):
-        z_copy(j).start()
-    tz[z] = us[...]
     lora_wait(3)
     unslot(3)
     obf[...] = acc[...].astype(bf16)
     out_copy = pltpu.make_async_copy(obf, out_hbm, osem.at[1])
     out_copy.start()
-    for k in range(NK):
-        for j in range(len(EX)):
-            ex_copy(k, j).wait_send()
-            lora_copy(k, j).wait_send()
-        for j in range(8):
-            g_copy(k, j).wait_send()
-        for j in range(len(XOFF)):
-            base_copy(k, j).wait_send()
-            c_copy(k, j).wait_send()
-        for s in range(4):
-            for up in ag_ways(k, s):
-                ag_copy(k, s, up).wait_send()
-    for j in range(len(XOFF)):
-        q_copy(j).wait_send()
-    for j in range(len(EX)):
-        y_copy(j).wait_send()
-    for j in range(len(ZOFF)):
-        z_copy(j).wait_recv()
-    st_ref[...] = jnp.where(row == NK, jnp.sum(tz[...], axis=0), squares)
-    for j in range(len(ZOFF)):
-        z_copy(j).wait_send()
+    left(snd.at[:, 0 : GROUP - 1], ex_s)
+    left(ls.at[:, 0 : GROUP - 1], l_s)
+    left(adb.at[:, 0 : NZ - 1], ag_s)
+    left(gs.at[:, 0 : NZ - 1], g_s)
+    left(bs, b_s)
+    left(far, f_s)
+    left(cr.at[:, 0 : NX - 1], c_s)
+    left(sqr.at[0 : NX - 1], q_s)
+    left(tz.at[0 : NZ - 1], z_s)
     grad_out.wait()
+    arrived(ty.at[0 : len(ALL)], y_r)
+    st_ref[...] = jnp.where(row == NK, jnp.sum(ty[...], axis=0), squares)
+    left(ty.at[0 : len(ALL)], y_s)
     out_copy.wait()
 
 
@@ -388,10 +395,11 @@
             jax.ShapeDtypeStruct(own, f32),
             jax.ShapeDtypeStruct((8, 128), f32),
         ),
-        in_specs=[vm, hbm, hbm, hbm, hbm],
+        in_specs=[hbm] * 5,
         out_specs=(hbm, hbm, vm),
         scratch_shapes=[
             pltpu.VMEM(own, f32),
+            pltpu.VMEM((1, tok), i32),
             pltpu.VMEM((1, tok), i32),
             pltpu.VMEM((tok, 128), i32),
             pltpu.VMEM((tok, 2 * fw), bf16),
@@ -399,8 +407,10 @@
             pltpu.VMEM((NK, GROUP, CHUNK, 2 * fw), bf16),
             pltpu.VMEM((NK, GROUP, CHUNK, 2 * fw), bf16),
             pltpu.VMEM((NK, NZ, 2, R, fw), bf16),
-            pltpu.VMEM((3, tok, fw), bf16),
-            pltpu.VMEM((3, tok, fw), bf16),
+            pltpu.VMEM((tok, fw), bf16),
+            pltpu.VMEM((2, tok // 2, fw), bf16),
+            pltpu.VMEM((2, tok, fw), bf16),
+            pltpu.VMEM((2, tok, fw), bf16),
             pltpu.VMEM((tok, fw), f32),
             pltpu.VMEM((NK, 2, GROUP * MOST, NZ * R), f32),
             pltpu.VMEM((NK, NX, 2, GROUP * MOST, NZ * R), f32),
@@ -409,27 +419,27 @@
             pltpu.VMEM((NK, NZ, 2, R, fw), bf16),
             pltpu.VMEM((NZ, 2, R, fw), f32),
             pltpu.VMEM((NK, 2, 2, R, fw), bf16),
-            pltpu.VMEM((NK, 2, 2, R, fw), bf16),
-            pltpu.VMEM((NK, 2, R, fw), bf16),
+            pltpu.VMEM((NK, 2, 3, R, fw), bf16),
             pltpu.VMEM((NK, 4, 2, R, fw), bf16),
             pltpu.VMEM(own, f32),
             pltpu.VMEM((tok, fw), bf16),
             pltpu.VMEM((8, 128), f32),
             pltpu.VMEM((NX, 8, 128), f32),
-            pltpu.VMEM((8, 128), f32),
-            pltpu.VMEM((GROUP, 8, 128), f32),
-            pltpu.VMEM((8, 128), f32),
-            pltpu.VMEM((NZ, 8, 128), f32),
-            dma((4,)), dma((2,)),
-            dma((NK, 7)), dma((NK, 7)),
-            dma((NK, 8)), dma((NK, 8)),
-            dma((NK, 3)), dma((NK, 3)),
-            dma((NK, 3)), dma((NK, 3)),
-            dma((NK, 7)), dma((NK, 7)),
-            dma((NK, 8)), dma((NK, 8)),
-            dma((3,)), dma((3,)),
-            dma((7,)), dma((7,)),
-            dma((7,)), dma((7,)),
+            pltpu.VMEM((1, 128), f32),
+            pltpu.VMEM((NX * GROUP, 1, 128), f32),
+            pltpu.VMEM((1, 128), f32),
+            pltpu.VMEM((NZ, 1, 128), f32),
+            dma((5,)), dma((2,)),
+            dma, dma((NK,)),
+            dma, dma((NK, 8)),
+            dma, dma((2,)),
+            dma, dma((NK,)),
+            dma, dma((NK,)),
+            dma, dma((NK,)),
+            dma, dma((NK,)), dma((NK, 2)),
+            dma, dma,
+            dma, dma,
+            dma, dma,
         ],
         compiler_params=pltpu.CompilerParams(
             collective_id=0, has_side_effects=True, vmem_limit_bytes=62 * 1024 * 1024

time: 88.5 us -> 85.2 us (0.963)
  Pallas kernels: 87.7 us -> 84.5 us
    pallas_call x1, Pallas kernels: 84.4 us -> 81.2 us  [local(): pl.pallas_call(kernel, out_shape=(jax.ShapeDtypeStruct((tok, fw), bf16),...]
where the time goes in v3:
time: 85.2 us; the launch traced here: 85.1 us
  Pallas kernels  84.5 us (99%)
    pallas_call x1, Pallas kernels, local(): pl.pallas_call(kernel, out_shape=(jax.ShapeDtypeStruct((tok, fw), bf16),...  81.2 us
    pallas_call x1, Pallas kernels, local(): pl.pallas_call(finish, out_shape=(jax.ShapeDtypeStruct((tok, fw), bf16),...  3.31 us

profile of v3, /device:TPU:1, one launch (start us, length us, event | category | flops | bytes accessed | tf_op | source)
XLA Modules:
  0.0 85.1 jit_solution(11017488375623725990)
XLA Ops:
  0.6 81.2 %shard_map.110 = (bf16[512,896]{1,0:T(8,128)(2,1)}, f32[4,2,16,896]{3,2,1,0:T(8,128)}, f32[8,128]{1,0:T(8,128)}) custom-call(s32[1,512]{1,0:T(1,128)} %bitcast.2, bf16[512,896]{1,0:T(8,128)(2,1)} %x_hbm.1, bf16[512,896]{1,0:T(8,128)(2,1)} %g_hbm.1, bf16[3584,896]{1,0:T(8,128)(2,1)} %w_hbm.1, f32[4,2,16,896]{3,2,1,0:T(8,128)} %ad_ref.1), custom_call_target="tpu_custom_call" | custom-call | tf_op jit(solution)/shard_map/pallas_call | solution.py:391
  81.8 3.3 %shard_map.111 = (bf16[512,896]{1,0:T(8,128)(2,1)}, f32[4,2,16,896]{3,2,1,0:T(8,128)}, f32[4,2,16,896]{3,2,1,0:T(8,128)}, f32[4,2,16,896]{3,2,1,0:T(8,128)}, f32[1,1]{1,0:T(1,128)}) custom-call(bf16[512,896]{1,0:T(8,128)(2,1)} %get-tuple-element.13.out_ref, f32[4,2,16,896]{3,2,1,0:T(8,128)} %get-tuple-element.14.grad_ref, ...), custom_call_target="tpu_custom_call" | custom-call | tf_op jit(solution)/shard_map/pallas_call | solution.py:448

commit v4 on v3

--- a/solution.py
+++ b/solution.py
@@ -21,6 +21,7 @@
 beta_second = 0.999
 adam_eps = 1e-08
 learn_rate = 0.01
+clip_limit = math.sqrt(2.0 * R * MODEL_WIDTH)
 bias_first = 1.0 - math.exp(1000.0 * math.log(beta_first))
 bias_second = 1.0 - math.exp(1000.0 * math.log(beta_second))
 
@@ -40,9 +41,9 @@
 
 
 def kernel(
-    ids_hbm, x_hbm, g_hbm, w_hbm, ad_hbm,
-    out_hbm, grad_hbm, st_ref,
-    adf, ids, posr, posc, xg, w, snd, rcv, adb, far, via, bs, br, acc, cs, cr, ls, lr, gs, gf, hs, hr, gr, gown, obf,
+    ids_hbm, x_hbm, g_hbm, w_hbm, ad_hbm, m_hbm, v_hbm,
+    out_hbm, na_hbm, nf_hbm, ns_hbm, st_ref,
+    adf, mb, vb, ids, posr, posc, xg, w, snd, rcv, adb, far, via, bs, br, acc, cs, cr, ls, lr, gs, gf, hs, hr, gr, gown, obf,
     sqs, sqr, ts, ty, us, tz,
     lsem, osem, ex_s, ex_r, ag_s, ag_r, f_s, f_r, b_s, b_r, c_s, c_r, l_s, l_r, g_s, g_r, h_r, q_s, q_r, y_s, y_r, z_s, z_r,
 ):
@@ -82,6 +83,8 @@
         pltpu.make_async_copy(x_hbm, xg.at[:, 0:fw], lsem.at[1]),
         pltpu.make_async_copy(g_hbm, xg.at[:, fw : 2 * fw], lsem.at[2]),
         pltpu.make_async_copy(w_hbm, w, lsem.at[3]),
+        pltpu.make_async_copy(m_hbm, mb, lsem.at[5]),
+        pltpu.make_async_copy(v_hbm, vb, lsem.at[6]),
     ]
     for cp in loads:
         cp.start()
@@ -265,7 +268,8 @@
     ag_pass(1, 0)
     for k in range(2, NK):
         adb[k, z] = adf[k].astype(bf16)
-    loads[4].wait()
+    for cp in loads[4:]:
+        cp.wait()
     frozen_far()
     ag_pass(0, 1)
     ag_pass(2, 0)
@@ -283,6 +287,7 @@
     ag_pass(3, 1)
     acc[...] = frozen_of(0, slice(None))
     ag_pass(0, 3)
+    frozen_near(0)
     ag_pass(2, 2)
     ag_pass(1, 3)
     ag_end(0)
@@ -294,6 +299,8 @@
             ag_end(k)
         arrived(rcv.at[k, 0 : GROUP - 1], ex_r.at[k])
         project(k)
+        if k + 1 < NK:
+            frozen_near(k + 1)
         if k == 0:
             ag_pass(3, 2)
             ag_pass(2, 3)
@@ -302,7 +309,6 @@
             hub(k - 1)
         arrived(cr.at[k, 0 : NX - 1], c_r.at[k])
         gradients(k)
-        frozen_near(k)
 
     def frozen(q):
         here = pl.ds(q * quarter, quarter)
@@ -335,8 +341,6 @@
         q_copy(j).start()
     sqr[x] = sq
     tz[z] = ts[...]
-    grad_out = pltpu.make_async_copy(gown, grad_hbm, osem.at[0])
-    grad_out.start()
     frozen(3)
     arrived(tz.at[0 : NZ - 1], z_r)
     us[...] = jnp.sum(tz[...], axis=0)
@@ -347,10 +351,25 @@
     unslot(2)
     arrived(sqr.at[0 : NX - 1], q_r)
     squares = sqr[0] + sqr[1] + sqr[2] + sqr[3]
+    for k in range(NK):
+        factor = clip_limit / jnp.maximum(jnp.sqrt(squares[k : k + 1, 0:1]), clip_limit)
+        clipped = gown[k] * factor
+        new_first = beta_first * mb[k] + (1.0 - beta_first) * clipped
+        new_second = beta_second * vb[k] + (1.0 - beta_second) * clipped * clipped
+        update = new_first / bias_first / (jnp.sqrt(new_second / bias_second) + adam_eps)
+        adf[k] = adf[k] - learn_rate * update
+        mb[k] = new_first
+        vb[k] = new_second
+    moved = [
+        pltpu.make_async_copy(src, dst, osem.at[i + 1])
+        for i, (src, dst) in enumerate(((adf, na_hbm), (mb, nf_hbm), (vb, ns_hbm)))
+    ]
+    for cp in moved:
+        cp.start()
     lora_wait(3)
     unslot(3)
     obf[...] = acc[...].astype(bf16)
-    out_copy = pltpu.make_async_copy(obf, out_hbm, osem.at[1])
+    out_copy = pltpu.make_async_copy(obf, out_hbm, osem.at[0])
     out_copy.start()
     left(snd.at[:, 0 : GROUP - 1], ex_s)
     left(ls.at[:, 0 : GROUP - 1], l_s)
@@ -361,43 +380,44 @@
     left(cr.at[:, 0 : NX - 1], c_s)
     left(sqr.at[0 : NX - 1], q_s)
     left(tz.at[0 : NZ - 1], z_s)
-    grad_out.wait()
     arrived(ty.at[0 : len(ALL)], y_r)
-    st_ref[...] = jnp.where(row == NK, jnp.sum(ty[...], axis=0), squares)
+    st_ref[...] = jnp.sum(ty[...], axis=0)
     left(ty.at[0 : len(ALL)], y_s)
-    out_copy.wait()
-
-
-def finish(out_ref, grad_ref, st_ref, ad_ref, m_ref, v_ref, o_ref, na_ref, nf_ref, ns_ref, norm_ref):
-    clip_limit = math.sqrt(2.0 * R * MODEL_WIDTH)
-    o_ref[...] = out_ref[...]
-    for k in range(NK):
-        factor = clip_limit / jnp.maximum(jnp.sqrt(st_ref[k : k + 1, 0:1]), clip_limit)
-        clipped = grad_ref[k] * factor
-        new_first = beta_first * m_ref[k] + (1.0 - beta_first) * clipped
-        new_second = beta_second * v_ref[k] + (1.0 - beta_second) * clipped * clipped
-        update = new_first / bias_first / (jnp.sqrt(new_second / bias_second) + adam_eps)
-        na_ref[k] = ad_ref[k] - learn_rate * update
-        nf_ref[k] = new_first
-        ns_ref[k] = new_second
-    norm_ref[...] = jnp.sqrt(st_ref[NK : NK + 1, 0:1])
+    for cp in (out_copy, *moved):
+        cp.wait()
+
+
+def finish(o_in, na_in, nf_in, ns_in, st_ref, o_out, na_out, nf_out, ns_out, norm_ref, sem):
+    moves = [
+        pltpu.make_async_copy(src, dst, sem.at[i])
+        for i, (src, dst) in enumerate(((na_in, na_out), (nf_in, nf_out), (ns_in, ns_out), (o_in, o_out)))
+    ]
+    for cp in moves:
+        cp.start()
+    norm_ref[...] = jnp.sqrt(st_ref[0:1, 0:1])
+    for cp in moves:
+        cp.wait()
 
 
 def local(inputs, cotangent, base_weight, adapter_ids, adapters, first_moment, second_moment):
     tok, fw = inputs.shape
     dma = pltpu.SemaphoreType.DMA
-    vm, hbm = pl.BlockSpec(memory_space=pltpu.VMEM), pl.BlockSpec(memory_space=pl.ANY)
+    vm, hbm, anywhere = (pl.BlockSpec(memory_space=m) for m in (pltpu.VMEM, pltpu.HBM, pl.ANY))
     own = (NK, 2, R, fw)
-    out, grads, stats = pl.pallas_call(
+    results = (
+        jax.ShapeDtypeStruct((tok, fw), bf16),
+        jax.ShapeDtypeStruct(own, f32),
+        jax.ShapeDtypeStruct(own, f32),
+        jax.ShapeDtypeStruct(own, f32),
+    )
+    *parts, stats = pl.pallas_call(
         kernel,
-        out_shape=(
-            jax.ShapeDtypeStruct((tok, fw), bf16),
-            jax.ShapeDtypeStruct(own, f32),
-            jax.ShapeDtypeStruct((8, 128), f32),
-        ),
-        in_specs=[hbm] * 5,
-        out_specs=(hbm, hbm, vm),
+        out_shape=(*results, jax.ShapeDtypeStruct((1, 128), f32)),
+        in_specs=[hbm] * 7,
+        out_specs=(anywhere,) * 4 + (vm,),
         scratch_shapes=[
+            pltpu.VMEM(own, f32),
+            pltpu.VMEM(own, f32),
             pltpu.VMEM(own, f32),
             pltpu.VMEM((1, tok), i32),
             pltpu.VMEM((1, tok), i32),
@@ -429,7 +449,7 @@
             pltpu.VMEM((NX * GROUP, 1, 128), f32),
             pltpu.VMEM((1, 128), f32),
             pltpu.VMEM((NZ, 1, 128), f32),
-            dma((5,)), dma((2,)),
+            dma((7,)), dma((4,)),
             dma, dma((NK,)),
             dma, dma((NK, 8)),
             dma, dma((2,)),
@@ -442,22 +462,17 @@
             dma, dma,
         ],
         compiler_params=pltpu.CompilerParams(
-            collective_id=0, has_side_effects=True, vmem_limit_bytes=62 * 1024 * 1024
+            collective_id=0, has_side_effects=True, vmem_limit_bytes=46 * 1024 * 1024
         ),
-    )(adapter_ids.reshape(1, tok), inputs, cotangent, base_weight, adapters)
+    )(*(pltpu.with_memory_space_constraint(t, pltpu.HBM) for t in (adapter_ids.reshape(1, tok), inputs, cotangent, base_weight, adapters, first_moment, second_moment)))
     out, new_adapters, new_first, new_second, norm = pl.pallas_call(
         finish,
-        out_shape=(
-            jax.ShapeDtypeStruct((tok, fw), bf16),
-            jax.ShapeDtypeStruct(own, f32),
-            jax.ShapeDtypeStruct(own, f32),
-            jax.ShapeDtypeStruct(own, f32),
-            jax.ShapeDtypeStruct((1, 1), f32),
-        ),
-        in_specs=[vm] * 6,
-        out_specs=(vm,) * 5,
-        compiler_params=pltpu.CompilerParams(vmem_limit_bytes=62 * 1024 * 1024),
-    )(out, grads, stats, adapters, first_moment, second_moment)
+        out_shape=(*results, jax.ShapeDtypeStruct((1, 1), f32)),
+        in_specs=[anywhere] * 4 + [vm],
+        out_specs=(hbm,) * 4 + (vm,),
+        scratch_shapes=[dma((4,))],
+        compiler_params=pltpu.CompilerParams(vmem_limit_bytes=8 * 1024 * 1024),
+    )(*parts, stats)
     return (out, new_adapters, new_first, new_second, norm.reshape(()))
 
 

time: 85.2 us -> 81.4 us (0.955)
  Pallas kernels: 84.5 us -> 80.7 us
    pallas_call x2, Pallas kernels: 84.5 us -> 80.7 us  [the longest x1 78.8 us: local(): pl.pallas_call(kernel, out_shape=(*results, jax.ShapeDtypeStruct((1, 128)...]
where the time goes in v4:
time: 81.4 us
  Pallas kernels  80.7 us (99%)
    pallas_call x1, Pallas kernels, local(): pl.pallas_call(kernel, out_shape=(*results, jax.ShapeDtypeStruct((1, 128)...  78.8 us
    pallas_call x1, Pallas kernels, local(): pl.pallas_call(finish, out_shape=(*results, jax.ShapeDtypeStruct((1, 1),...  1.92 us

profile of v4, /device:TPU:1, one launch (start us, length us, event | category | flops | bytes accessed | tf_op | source)
XLA Modules:
  0.0 81.4 jit_solution(3187453140301315540)
XLA Ops:
  0.6 78.8 %shard_map.110 = (bf16[512,896]{1,0:T(8,128)(2,1)S(1)}, f32[4,2,16,896]{3,2,1,0:T(8,128)S(1)}, f32[4,2,16,896]{3,2,1,0:T(8,128)S(1)}, f32[4,2,16,896]{3,2,1,0:T(8,128)S(1)}, f32[1,128]{1,0:T(1,128)S(1)}) custom-call(s32[1,512]{1,0:T(1,128)} %bitcast.2, bf16[512,896]{1,0:T(8,128)(2,1)} %x_hbm.1, bf16[512,896]{1,0:T(8,128)(2,1)} %g_hbm.1, ...), custom_call_target="tpu_custom_call" | custom-call | tf_op jit(solution)/shard_map/pallas_call | solution.py:413
  79.4 1.9 %shard_map.111 = (bf16[512,896]{1,0:T(8,128)(2,1)}, f32[4,2,16,896]{3,2,1,0:T(8,128)}, f32[4,2,16,896]{3,2,1,0:T(8,128)}, f32[4,2,16,896]{3,2,1,0:T(8,128)}, f32[1,1]{1,0:T(1,128)}) custom-call(bf16[512,896]{1,0:T(8,128)(2,1)S(1)} %get-tuple-element.15.o_in, f32[4,2,16,896]{3,2,1,0:T(8,128)S(1)} %get-tuple-element.16.na_in, ...), custom_call_target="tpu_custom_call" | custom-call | tf_op jit(solution)/shard_map/pallas_call | solution.py:468

commit v5 on v4

--- a/solution.py
+++ b/solution.py
@@ -25,7 +25,7 @@
 bias_first = 1.0 - math.exp(1000.0 * math.log(beta_first))
 bias_second = 1.0 - math.exp(1000.0 * math.log(beta_second))
 
-EX = ((2, 0), (2, 1), (1, 0), (3, 0), (1, 1), (3, 1), (0, 1))
+EX = ((2, 0), (1, 0), (3, 0), (2, 1), (1, 1), (3, 1), (0, None))
 ZOFF = (4, 3, 5, 2, 6, 1, 7)
 XOFF = (2, 1, 3)
 ALL = tuple((dy, dc, dx) for dy in (2, 1, 3, 0) for dx in (2, 1, 3, 0) for dc in (1, 0) if (dy, dc, dx) != (0, 0, 0))
@@ -55,8 +55,8 @@
     nrow = GROUP * CHUNK
     quarter = tok // NK
 
-    def at_yc(dy, dc):
-        yy, cc = (y + dy) % NY, (c + dc) % NC
+    def at_yc(dy, core):
+        yy, cc = (y + dy) % NY, 1 - c if core is None else core
         return yy * NC + cc, ((yy * NZ + z) * NC + cc, x)
 
     def at_z(dz):
@@ -293,8 +293,6 @@
     ag_end(0)
 
     for k in range(NK):
-        if k == NK - 1:
-            hub(k - 1)
         if k > 0:
             ag_end(k)
         arrived(rcv.at[k, 0 : GROUP - 1], ex_r.at[k])
@@ -305,7 +303,7 @@
             ag_pass(3, 2)
             ag_pass(2, 3)
             ag_pass(3, 3)
-        elif k < NK - 1:
+        else:
             hub(k - 1)
         arrived(cr.at[k, 0 : NX - 1], c_r.at[k])
         gradients(k)

time: 81.4 us -> 79.2 us (0.973)
  Pallas kernels: 80.7 us -> 78.4 us
    pallas_call x1, Pallas kernels: 78.8 us -> 76.5 us  [local(): pl.pallas_call(kernel, out_shape=(*results, jax.ShapeDtypeStruct((1, 128)...]
where the time goes in v5:
time: 79.2 us; the launch traced here: 79.1 us
  Pallas kernels  78.4 us (99%)
    pallas_call x1, Pallas kernels, local(): pl.pallas_call(kernel, out_shape=(*results, jax.ShapeDtypeStruct((1, 128)...  76.5 us
    pallas_call x1, Pallas kernels, local(): pl.pallas_call(finish, out_shape=(*results, jax.ShapeDtypeStruct((1, 1),...  1.92 us

profile of v5, /device:TPU:1, one launch (start us, length us, event | category | flops | bytes accessed | tf_op | source)
XLA Modules:
  0.0 79.1 jit_solution(12035679557911483704)
XLA Ops:
  0.6 76.5 %shard_map.110 = (bf16[512,896]{1,0:T(8,128)(2,1)S(1)}, f32[4,2,16,896]{3,2,1,0:T(8,128)S(1)}, f32[4,2,16,896]{3,2,1,0:T(8,128)S(1)}, f32[4,2,16,896]{3,2,1,0:T(8,128)S(1)}, f32[1,128]{1,0:T(1,128)S(1)}) custom-call(s32[1,512]{1,0:T(1,128)} %bitcast.2, bf16[512,896]{1,0:T(8,128)(2,1)} %x_hbm.1, bf16[512,896]{1,0:T(8,128)(2,1)} %g_hbm.1, ...), custom_call_target="tpu_custom_call" | custom-call | tf_op jit(solution)/shard_map/pallas_call | solution.py:411
  77.1 1.9 %shard_map.111 = (bf16[512,896]{1,0:T(8,128)(2,1)}, f32[4,2,16,896]{3,2,1,0:T(8,128)}, f32[4,2,16,896]{3,2,1,0:T(8,128)}, f32[4,2,16,896]{3,2,1,0:T(8,128)}, f32[1,1]{1,0:T(1,128)}) custom-call(bf16[512,896]{1,0:T(8,128)(2,1)S(1)} %get-tuple-element.15.o_in, f32[4,2,16,896]{3,2,1,0:T(8,128)S(1)} %get-tuple-element.16.na_in, ...), custom_call_target="tpu_custom_call" | custom-call | tf_op jit(solution)/shard_map/pallas_call | solution.py:466

commit v6 on v5

--- a/solution.py
+++ b/solution.py
@@ -220,11 +220,11 @@
         proj = jnp.where(mine, low[1][:, None, :], 0.0).reshape(nrow, NZ * R)
         for i, (side, first) in enumerate(((pull, 0), (proj, fw))):
             grad = (adapter_scale * nn(side.T.astype(bf16), rows_of(k, first))).reshape(NZ, R, fw)
-            gf[:, i] = grad
+            gf[k % 2, :, i] = grad
             gs[k, :, i] = grad.astype(bf16)
         for j in (2, 3, 4, 5, 0, 1):
             g_copy(k, j).start()
-        gown[k] = gf[z]
+        gown[k] = gf[k % 2, z]
         lora = adapter_scale * nn(pull.astype(bf16), adb[k, :, 0].reshape(NZ * R, fw))
         ls[k] = lora.astype(bf16).reshape(GROUP, CHUNK, fw)
         for j in range(len(EX)):
@@ -236,7 +236,7 @@
             arrived(hr.at[k, side], h_r.at[k, side])
             sign = 1 if side == 0 else -1
             for i in range(2):
-                t = gf[at_z(2 * sign)[0], i] + hr[k, side, i].astype(f32)
+                t = gf[k % 2, at_z(2 * sign)[0], i] + hr[k, side, i].astype(f32)
                 if i == side:
                     t = t + hr[k, side, 2].astype(f32)
                 hs[k, side, i] = t.astype(bf16)
@@ -303,10 +303,12 @@
             ag_pass(3, 2)
             ag_pass(2, 3)
             ag_pass(3, 3)
-        else:
+        elif k < NK - 1:
             hub(k - 1)
         arrived(cr.at[k, 0 : NX - 1], c_r.at[k])
         gradients(k)
+        if k == NK - 1:
+            hub(k - 1)
 
     def frozen(q):
         here = pl.ds(q * quarter, quarter)
@@ -435,7 +437,7 @@
             pltpu.VMEM((NK, GROUP, CHUNK, fw), bf16),
             pltpu.VMEM((NK, GROUP, CHUNK, fw), bf16),
             pltpu.VMEM((NK, NZ, 2, R, fw), bf16),
-            pltpu.VMEM((NZ, 2, R, fw), f32),
+            pltpu.VMEM((2, NZ, 2, R, fw), f32),
             pltpu.VMEM((NK, 2, 2, R, fw), bf16),
             pltpu.VMEM((NK, 2, 3, R, fw), bf16),
             pltpu.VMEM((NK, 4, 2, R, fw), bf16),

time: 79.2 us -> 77 us (0.972)
  Pallas kernels: 78.4 us -> 76.3 us
    pallas_call x1, Pallas kernels: 76.5 us -> 74.4 us  [local(): pl.pallas_call(kernel, out_shape=(*results, jax.ShapeDtypeStruct((1, 128)...]
where the time goes in v6:
time: 77 us
  Pallas kernels  76.3 us (99%)
    pallas_call x1, Pallas kernels, local(): pl.pallas_call(kernel, out_shape=(*results, jax.ShapeDtypeStruct((1, 128)...  74.4 us
    pallas_call x1, Pallas kernels, local(): pl.pallas_call(finish, out_shape=(*results, jax.ShapeDtypeStruct((1, 1),...  1.92 us

profile of v6, /device:TPU:1, one launch (start us, length us, event | category | flops | bytes accessed | tf_op | source)
XLA Modules:
  0.0 77.0 jit_solution(8634386500013088445)
XLA Ops:
  0.6 74.4 %shard_map.110 = (bf16[512,896]{1,0:T(8,128)(2,1)S(1)}, f32[4,2,16,896]{3,2,1,0:T(8,128)S(1)}, f32[4,2,16,896]{3,2,1,0:T(8,128)S(1)}, f32[4,2,16,896]{3,2,1,0:T(8,128)S(1)}, f32[1,128]{1,0:T(1,128)S(1)}) custom-call(s32[1,512]{1,0:T(1,128)} %bitcast.2, bf16[512,896]{1,0:T(8,128)(2,1)} %x_hbm.1, bf16[512,896]{1,0:T(8,128)(2,1)} %g_hbm.1, ...), custom_call_target="tpu_custom_call" | custom-call | tf_op jit(solution)/shard_map/pallas_call | solution.py:413
  75.0 1.9 %shard_map.111 = (bf16[512,896]{1,0:T(8,128)(2,1)}, f32[4,2,16,896]{3,2,1,0:T(8,128)}, f32[4,2,16,896]{3,2,1,0:T(8,128)}, f32[4,2,16,896]{3,2,1,0:T(8,128)}, f32[1,1]{1,0:T(1,128)}) custom-call(bf16[512,896]{1,0:T(8,128)(2,1)S(1)} %get-tuple-element.15.o_in, f32[4,2,16,896]{3,2,1,0:T(8,128)S(1)} %get-tuple-element.16.na_in, ...), custom_call_target="tpu_custom_call" | custom-call | tf_op jit(solution)/shard_map/pallas_call | solution.py:468
